TPU v7x, 256 devices: a whole 4x4x8 slice. The times are simulated.
256 devices in a mesh: section: 8 (over y, core), expert: 32 (over z, x).
Axes of the slice: x: 4, y: 4, z: 8, core: 2. Of those that a mesh axis runs over, the one named last changes fastest.
Arguments:
- inputs: bfloat16 [8, 4096, 1024], P('section', 'expert'), may hold values from -6 to 6
- out_grads: bfloat16 [8, 4096, 1024], P('section', 'expert'), may hold values from -6 to 6
- expert_ids: int32 [8, 4096, 8], P('section', 'expert'), may hold values from 0 to 63, all different within a row; in each aligned block of 128 rows (0 to 127, 128 to 255, ..., all dimensions but the last counted through in order) at most 24 rows name the same one
- route_levels: int32 [8, 4096, 8], P('section', 'expert'), may hold values from 8 to 256
- w_gate: bfloat16 [8, 64, 1024, 384], P('section', 'expert'), may hold values from -0.1875 to 0.1875
- w_up: bfloat16 [8, 64, 1024, 384], P('section', 'expert'), may hold values from -0.1875 to 0.1875
- w_down: bfloat16 [8, 64, 384, 1024], P('section', 'expert'), may hold values from -0.3125 to 0.3125
Outputs:
- upstream: bfloat16 [8, 4096, 1024], P('section', 'expert')
- route_grad: bfloat16 [8, 4096, 8], P('section', 'expert')
- gate_update: bfloat16 [8, 64, 1024, 384], P('section', 'expert')
- up_update: bfloat16 [8, 64, 1024, 384], P('section', 'expert')
- down_update: bfloat16 [8, 64, 384, 1024], P('section', 'expert')
Inputs may be any that keep to these rules, and one draw needn't show every extreme that they name: `expert_ids`: each token names 8 different experts; among the 128 tokens of one aligned block no expert is named more than 24 times.
All inputs are finite; a program needn't handle non-finite values.
Results may differ from a plain program's by a relative error of at most 0.0064.
Values may be sent and summed in bfloat16 or wider, within the bound.
A program may use at most 128 MiB of HBM per device.

v0:
```python
import math

import jax
import jax.numpy as jnp
from jax import lax
from jax.sharding import PartitionSpec as P


def in_one_piece(arrays, axis, split_dim, concat_dim, along):
    widths = [math.prod(a.shape[along:]) for a in arrays]
    both = jnp.concatenate(
        [a.reshape(*a.shape[:along], w) for a, w in zip(arrays, widths)], axis=along
    )
    whole = lax.all_to_all(both, axis, split_axis=split_dim, concat_axis=concat_dim, tiled=True)
    blocks = jnp.split(whole, [sum(widths[:k]) for k in range(1, len(widths))], axis=along)
    return tuple(
        (b.reshape(*whole.shape[:along], *a.shape[along:]) for a, b in zip(arrays, blocks))
    )


def shifted(value, axis, by):
    size = lax.axis_size(axis)
    pairs = [(i, i + by) for i in range(size) if 0 <= i + by < size]
    return lax.ppermute(value, axis, pairs)


def flat_slots(expert_ids, experts_all, capacity):
    blocks = expert_ids.shape[0]
    flat_ids = expert_ids.reshape(blocks, -1)
    catalog = jnp.arange(experts_all, dtype=jnp.int32)
    onehot = (flat_ids[:, :, None] == catalog[None, None, :]).astype(jnp.int32)
    rank_table = jnp.cumsum(onehot, axis=1) - 1
    slot_of = jnp.sum(onehot * rank_table, axis=2)
    return (flat_ids * capacity + slot_of).reshape(expert_ids.shape)


def expert_backward(slot_inputs, slot_grads, slot_routes, w_gate, w_up, w_down):
    gate_pre = jnp.einsum("esd,edh->esh", slot_inputs, w_gate, preferred_element_type=jnp.float32)
    up_pre = jnp.einsum("esd,edh->esh", slot_inputs, w_up, preferred_element_type=jnp.float32)
    sigmoid_gate = jax.nn.sigmoid(gate_pre)
    silu_gate = gate_pre * sigmoid_gate
    active = (silu_gate * up_pre).astype(jnp.bfloat16)
    expert_out = jnp.einsum("esh,ehd->esd", active, w_down, preferred_element_type=jnp.float32)
    route_part = jnp.sum(slot_grads.astype(jnp.float32) * expert_out, axis=2).astype(jnp.bfloat16)
    weighted = (
        slot_routes.astype(jnp.float32)[:, :, None] * slot_grads.astype(jnp.float32)
    ).astype(jnp.bfloat16)
    active_grad = jnp.einsum("esd,ehd->esh", weighted, w_down, preferred_element_type=jnp.float32)
    gate_pre_grad = (
        active_grad * up_pre * sigmoid_gate * (1.0 + gate_pre * (1.0 - sigmoid_gate))
    ).astype(jnp.bfloat16)
    up_pre_grad = (active_grad * silu_gate).astype(jnp.bfloat16)
    input_grad = (
        jnp.einsum("esh,edh->esd", gate_pre_grad, w_gate, preferred_element_type=jnp.float32)
        + jnp.einsum("esh,edh->esd", up_pre_grad, w_up, preferred_element_type=jnp.float32)
    ).astype(jnp.bfloat16)
    down_part = jnp.einsum(
        "esh,esd->ehd", active, weighted, preferred_element_type=jnp.float32
    ).astype(jnp.bfloat16)
    gate_part = jnp.einsum(
        "esd,esh->edh", slot_inputs, gate_pre_grad, preferred_element_type=jnp.float32
    ).astype(jnp.bfloat16)
    up_part = jnp.einsum(
        "esd,esh->edh", slot_inputs, up_pre_grad, preferred_element_type=jnp.float32
    ).astype(jnp.bfloat16)
    return (input_grad, route_part, gate_part, up_part, down_part)


def body(inputs, out_grads, expert_ids, route_levels, w_gate, w_up, w_down):
    tok_rows = inputs.shape[1]
    width = inputs.shape[2]
    top_count = expert_ids.shape[2]
    experts_local = w_gate.shape[1]
    groups = lax.axis_size("expert")
    experts_all = experts_local * groups
    capacity = 3 * tok_rows * top_count // (2 * experts_all)
    slot_total = experts_all * capacity
    own_index = flat_slots(expert_ids[0][None], experts_all, capacity)[0]
    catalog = jnp.arange(slot_total, dtype=jnp.int32)
    select = (own_index[:, :, None] == catalog).astype(jnp.bfloat16)
    placing = jnp.sum(select, axis=1)
    route_values = (route_levels[0].astype(jnp.float32) / 256.0).astype(jnp.bfloat16)
    send_inputs = (
        jnp.einsum("ts,td->sd", placing, inputs[0], preferred_element_type=jnp.float32)
        .astype(jnp.bfloat16)
        .reshape(experts_all, capacity, width)
    )
    send_grads = (
        jnp.einsum("ts,td->sd", placing, out_grads[0], preferred_element_type=jnp.float32)
        .astype(jnp.bfloat16)
        .reshape(experts_all, capacity, width)
    )
    send_routes = (
        jnp.einsum("tks,tk->s", select, route_values, preferred_element_type=jnp.float32)
        .astype(jnp.bfloat16)
        .reshape(experts_all, capacity)
    )
    slot_inputs, slot_grads, slot_routes = in_one_piece(
        (send_inputs, send_grads, send_routes), "expert", 0, 1, 2
    )
    input_grad, route_part, gate_part, up_part, down_part = expert_backward(
        slot_inputs, slot_grads, slot_routes, w_gate[0], w_up[0], w_down[0]
    )
    back_inputs, back_routes = (
        lax.all_to_all(input_grad, "expert", split_axis=1, concat_axis=0, tiled=True),
        lax.all_to_all(route_part, "expert", split_axis=1, concat_axis=0, tiled=True),
    )
    token_grad = jnp.dot(
        placing, back_inputs.reshape(slot_total, width), preferred_element_type=jnp.float32
    ).astype(jnp.bfloat16)
    token_route = jnp.einsum(
        "tks,s->tk", select, back_routes.reshape(slot_total), preferred_element_type=jnp.float32
    ).astype(jnp.bfloat16)
    upstream = shifted(token_grad, "section", -1)
    return (upstream[None], token_route[None], gate_part[None], up_part[None], down_part[None])


def solution(mesh):
    in_specs = (
        P("section", "expert", None),
        P("section", "expert", None),
        P("section", "expert", None),
        P("section", "expert", None),
        P("section", "expert", None, None),
        P("section", "expert", None, None),
        P("section", "expert", None, None),
    )
    out_specs = (
        P("section", "expert", None),
        P("section", "expert", None),
        P("section", "expert", None, None),
        P("section", "expert", None, None),
        P("section", "expert", None, None),
    )
    return jax.shard_map(body, mesh=mesh, in_specs=in_specs, out_specs=out_specs, check_vma=False)
```

profile of v0, /device:TPU:1, one launch (start us, length us, event | category | flops | bytes accessed | tf_op | source)
XLA Modules:
  0.0 317.3 jit_solution(10611958678711964622)
XLA Ops:
  0.6 0.0 copy-start
  0.6 0.9 copy.52
  1.6 0.1 eq.40
  1.7 18.0 %reduce-window.6 = s32[1,64,8,128]{3,2,1,0:T(8,128)S(1)} reduce-window(s32[1,64,8,128]{3,2,1,0:T(8,128)S(1)} %bitcast.92, s32[]{:T(128)} %constant.14.clone.1), window={size=1x1x1x128 pad=0_0x0_0x0_0x127_0}, to_apply=%region_0.0 | reduce-window | flops 8323072 | bytes 524292 | tf_op jit(solution)/shard_map/reduce-window
  19.7 0.1 slice.8
  19.9 0.7 fusion.50
  20.6 0.1 copy.65
  20.8 0.1 copy.54
  20.9 0.1 copy.55
  21.0 0.1 broadcast.67
  21.2 0.1 fusion.49
  21.3 0.1 reduce_sum.33
  21.4 0.0 copy-start.6
  21.4 3.1 fusion.5
  24.5 0.0 copy-done.6
  24.5 0.0 copy-start.8
  24.6 1.2 fusion.46
  25.8 0.0 copy-start.9
  25.8 0.7 reshape_reshape.4
  26.5 0.0 copy-done.8
  26.5 1.0 convolution_convert_fusion
  27.5 0.0 copy-done.9
  27.5 1.0 convolution_convert_fusion.1
  28.5 0.6 pad_maximum_fusion
  29.1 160.3 %all_to_all.46 = bf16[64,24,2049]{2,1,0:T(8,128)(2,1)S(1)} all-to-all(bf16[64,24,2049]{2,1,0:T(8,128)(2,1)S(1)} %pad_maximum_fusion), channel_id=1, replica_groups=mesh['section'=8,'expert'=32] {'expert'}, dimensions={0} | all-to-all | bytes 12589056 | tf_op jit(solution)/shard_map/all_to_all | solution.py:14
  189.4 0.5 copy.57
  189.8 0.0 copy-start.1
  189.8 0.2 convert_reduce_fusion
  190.0 0.0 copy-start.12
  190.0 4.5 %fusion.17 = f32[2,768,384]{2,1,0:T(8,128)S(1)} fusion(bf16[2,768,2049]{2,1,0:T(8,128)(2,1)S(1)} %bitcast.85, bf16[1,2,1024,384]{3,2,1,0:T(8,128)(2,1)} %param.11), kind=kOutput, calls=%fused_computation.26 | convolution fusion | flops 1207959552 | bytes 7077888 | tf_op jit(solution)/shard_map/esd,edh->esh/dot_general | solution.py:38
  194.5 0.0 copy-done.10
  194.5 0.0 copy-done.12
  194.6 1.9 fusion.10
  196.4 0.0 copy-done
  196.4 3.8 %multiply_convert_fusion = (bf16[2,768,384]{2,1,0:T(8,128)(2,1)S(1)}, bf16[2,768,384]{2,1,0:T(8,128)(2,1)}, bf16[2,768,384]{2,1,0:T(8,128)(2,1)}) fusion(f32[2,768,384]{2,1,0:T(8,128)S(1)} %fusion.17, f32[2,768,384]{2,1,0:T(8,128)S(1)} %fusion.10, bf16[1,2,1024,384]{3,2,1,0:T(8,128)(2,1)S(1)} %copy-done, bf16[2,768,2049]{2,1,0:T(8,128)(2,1)S(1)} %bitcast.87), kind=kOutput, calls=%fused_computation.17 | convolution fusion | flops 1216806912 | bytes 12976128 | tf_op jit(solution)/shard_map/esd,edh->esh/dot_general | solution.py:39
  200.3 0.0 copy-done.1
  200.3 1.1 copy-done.13
  201.3 2.5 fusion.1
  203.8 0.8 convert_element_type.91
  204.6 0.6 copy.61
  205.2 5.1 %all-to-all-start.2 = ((bf16[2,32,24]{2,0,1:T(2,128)(2,1)}), bf16[2,32,24]{2,0,1:T(2,128)(2,1)S(1)}, u32[]{:S(2)}, u32[]{:S(2)}) async-start(bf16[2,32,24]{2,0,1:T(2,128)(2,1)} %copy.61), calls=%async_computation.2 | async-start | bytes 32768 | tf_op jit(solution)/shard_map/all_to_all | solution.py:106
  210.3 0.0 copy-done.2
  210.3 0.0 copy-start.3
  210.4 3.2 %fusion.30 = f32[2,768,1024]{2,1,0:T(8,128)S(1)} fusion(bf16[2,768,384]{2,1,0:T(8,128)(2,1)} %get-tuple-element.6, bf16[1,2,1024,384]{3,2,1,0:T(8,128)(2,1)S(1)} %copy-done.2), kind=kOutput, calls=%fused_computation.33 | convolution fusion | flops 1207959552 | bytes 9043968 | tf_op jit(solution)/shard_map/esh,edh->esd/dot_general | solution.py:54
  213.6 1.8 add_convert_fusion
  215.4 4.9 %copy.58 = bf16[2,768,1024]{2,0,1:T(2,128)(2,1)} copy(bf16[2,768,1024]{2,1,0:T(8,128)(2,1)S(1)} %add_convert_fusion) | data formatting | bytes 6291456 | tf_op jit(solution)/shard_map/convert_element_type | solution.py:56
  220.3 0.0 all-to-all-done.2
  220.3 9.7 %all-to-all-start.1 = ((bf16[2,768,1024]{2,0,1:T(2,128)(2,1)}), bf16[2,768,1024]{2,0,1:T(2,128)(2,1)}, u32[]{:S(2)}, u32[]{:S(2)}) async-start(bf16[2,768,1024]{2,0,1:T(2,128)(2,1)} %copy.58), calls=%async_computation.1 | async-start | bytes 6291456 | tf_op jit(solution)/shard_map/all_to_all | solution.py:105
  230.0 0.0 copy-start.4
  230.0 5.0 %fusion.43 = bf16[1,2,1024,384]{3,2,1,0:T(8,128)(2,1)} fusion(bf16[2,768,384]{2,1,0:T(8,128)(2,1)S(1)} %copy-done.5, bf16[2,768,2049]{2,1,0:T(8,128)(2,1)} %bitcast.89), kind=kOutput, calls=%fused_computation.42 | convolution fusion | flops 1208745984 | bytes 5898240 | tf_op jit(solution)/shard_map/esd,esh->edh/dot_general | solution.py:60
  235.0 5.0 %fusion.40 = bf16[1,2,1024,384]{3,2,1,0:T(8,128)(2,1)} fusion(bf16[2,768,384]{2,1,0:T(8,128)(2,1)S(1)} %copy-done.4, bf16[2,768,2049]{2,1,0:T(8,128)(2,1)} %bitcast.90), kind=kOutput, calls=%fused_computation.41 | convolution fusion | flops 1208745984 | bytes 5898240 | tf_op jit(solution)/shard_map/esd,esh->edh/dot_general | solution.py:63
  240.0 4.6 %fusion.37 = bf16[1,2,384,1024]{3,2,1,0:T(8,128)(2,1)} fusion(bf16[2,768,384]{2,1,0:T(8,128)(2,1)S(1)} %copy-done.14, f32[2,768]{1,0:T(2,128)S(1)} %copy-done.11, bf16[2,768,2049]{2,1,0:T(8,128)(2,1)} %bitcast.91), kind=kOutput, calls=%fused_computation.40 | convolution fusion | flops 1213464576 | bytes 5904384 | tf_op jit(solution)/shard_map/esh,esd->ehd/dot_general | solution.py:57
  244.6 0.1 reshape.181
  244.7 55.5 %all-to-all-done.1 = bf16[2,768,1024]{2,0,1:T(2,128)(2,1)} async-done(((bf16[2,768,1024]{2,0,1:T(2,128)(2,1)}), bf16[2,768,1024]{2,0,1:T(2,128)(2,1)}, u32[]{:S(2)}, u32[]{:S(2)}) %all-to-all-start.1) | async-done | bytes 3145760 | tf_op jit(solution)/shard_map/all_to_all | solution.py:105
  300.2 2.8 copy.59
  303.1 0.4 copy.60
  303.5 0.0 copy-start.7
  303.5 0.6 convolution_convert_fusion.2
  304.1 4.7 %collective-permute-start = (bf16[128,1024]{1,0:T(8,128)(2,1)S(1)}, bf16[128,1024]{1,0:T(8,128)(2,1)S(1)}, u32[]{:S(2)}, u32[]{:S(2)}) collective-permute-start(bf16[128,1024]{1,0:T(8,128)(2,1)S(1)} %convolution_convert_fusion.2), channel_id=1, source_target_pairs={{32,0},{64,32},{96,64},{128,96},{160,128},{192,160},{224,192},{33,... | collective-permute-start | bytes 786440 | tf_op jit(solution)/shard_map/ppermute | solution.py:24
  308.8 7.1 %fusion.2 = bf16[1,128,8]{2,0,1:T(2,128)(2,1)S(1)} fusion(bf16[1536,1,1]{0,1,2:T(2,128)(2,1)S(1)} %reshape.181, s32[128,8]{1,0:T(8,128)S(1)} %copy-done.7), kind=kOutput, calls=%fused_computation.7 | convolution fusion | flops 4718592 | bytes 9216 | tf_op jit(solution)/shard_map/tks,s->tk/dot_general | solution.py:111
  315.9 0.1 copy.66
  316.0 0.6 fusion.51
  316.6 0.0 collective-permute-done
  316.6 0.7 copy.72
  (19 shorter events, 0.2 us)
Async XLA Ops:
  0.6 195.8 %copy-start = (bf16[1,2,1024,384]{3,2,1,0:T(8,128)(2,1)S(1)}, bf16[1,2,1024,384]{3,2,1,0:T(8,128)(2,1)}, u32[]{:S(2)}) copy-start(bf16[1,2,1024,384]{3,2,1,0:T(8,128)(2,1)} %param.12) | copy-start | bytes 4718596
  21.4 3.1 copy-start.6
  24.5 2.0 copy-start.8
  25.8 1.7 copy-start.9
  189.8 10.4 %copy-start.1 = (bf16[32,2,24,2049]{3,2,0,1:T(8,128)(2,1)}, bf16[32,2,24,2049]{3,2,0,1:T(8,128)(2,1)S(1)}, u32[]{:S(2)}) copy-start(bf16[32,2,24,2049]{3,2,0,1:T(8,128)(2,1)S(1)} %copy.57) | copy-start | bytes 18883588
  190.0 4.5 %copy-start.10 = (f32[2,768]{1,0:T(2,128)}, f32[2,768]{1,0:T(2,128)S(1)}, u32[]{:S(2)}) copy-start(f32[2,768]{1,0:T(2,128)S(1)} %convert_reduce_fusion) | copy-start | bytes 18436
  190.0 4.5 %copy-start.12 = (bf16[1,2,384,1024]{3,2,1,0:T(8,128)(2,1)S(1)}, bf16[1,2,384,1024]{3,2,1,0:T(8,128)(2,1)}, u32[]{:S(2)}) copy-start(bf16[1,2,384,1024]{3,2,1,0:T(8,128)(2,1)} %param.13) | copy-start | bytes 4718596
  200.3 1.1 copy-start.13
  201.3 9.0 %copy-start.2 = (bf16[1,2,1024,384]{3,2,1,0:T(8,128)(2,1)S(1)}, bf16[1,2,1024,384]{3,2,1,0:T(8,128)(2,1)}, u32[]{:S(2)}) copy-start(bf16[1,2,1024,384]{3,2,1,0:T(8,128)(2,1)} %param.11) | copy-start | bytes 4718596
  205.2 15.1 %all-to-all-start.2 = ((bf16[2,32,24]{2,0,1:T(2,128)(2,1)}), bf16[2,32,24]{2,0,1:T(2,128)(2,1)S(1)}, u32[]{:S(2)}, u32[]{:S(2)}) async-start(bf16[2,32,24]{2,0,1:T(2,128)(2,1)} %copy.61), calls=%async_computation.2 | async-start | bytes 32768 | tf_op jit(solution)/shard_map/all_to_all | solution.py:106
  210.3 3.2 %copy-start.3 = (bf16[2,768,384]{2,1,0:T(8,128)(2,1)S(1)}, bf16[2,768,384]{2,1,0:T(8,128)(2,1)}, u32[]{:S(2)}) copy-start(bf16[2,768,384]{2,1,0:T(8,128)(2,1)} %get-tuple-element.7) | copy-start | bytes 3538948
  220.3 9.7 %copy-start.5 = (bf16[2,768,384]{2,1,0:T(8,128)(2,1)S(1)}, bf16[2,768,384]{2,1,0:T(8,128)(2,1)}, u32[]{:S(2)}) copy-start(bf16[2,768,384]{2,1,0:T(8,128)(2,1)} %get-tuple-element.6) | copy-start | bytes 3538948
  220.3 79.9 %all-to-all-start.1 = ((bf16[2,768,1024]{2,0,1:T(2,128)(2,1)}), bf16[2,768,1024]{2,0,1:T(2,128)(2,1)}, u32[]{:S(2)}, u32[]{:S(2)}) async-start(bf16[2,768,1024]{2,0,1:T(2,128)(2,1)} %copy.58), calls=%async_computation.1 | async-start | bytes 6291456 | tf_op jit(solution)/shard_map/all_to_all | solution.py:105
  230.0 5.0 %copy-start.4 = (bf16[2,768,384]{2,1,0:T(8,128)(2,1)S(1)}, bf16[2,768,384]{2,1,0:T(8,128)(2,1)}, u32[]{:S(2)}) copy-start(bf16[2,768,384]{2,1,0:T(8,128)(2,1)} %get-tuple-element.7) | copy-start | bytes 3538948
  235.0 5.0 %copy-start.11 = (f32[2,768]{1,0:T(2,128)S(1)}, f32[2,768]{1,0:T(2,128)}, u32[]{:S(2)}) copy-start(f32[2,768]{1,0:T(2,128)} %copy-done.10) | copy-start | bytes 18436
  235.0 5.0 %copy-start.14 = (bf16[2,768,384]{2,1,0:T(8,128)(2,1)S(1)}, bf16[2,768,384]{2,1,0:T(8,128)(2,1)}, u32[]{:S(2)}) copy-start(bf16[2,768,384]{2,1,0:T(8,128)(2,1)} %copy-done.13) | copy-start | bytes 3538948
  303.5 5.3 %copy-start.7 = (s32[128,8]{1,0:T(8,128)S(1)}, s32[128,8]{1,0:T(8,128)}, u32[]{:S(2)}) copy-start(s32[128,8]{1,0:T(8,128)} %copy-done.6) | copy-start | bytes 12292
  304.1 12.5 %collective-permute-start = (bf16[128,1024]{1,0:T(8,128)(2,1)S(1)}, bf16[128,1024]{1,0:T(8,128)(2,1)S(1)}, u32[]{:S(2)}, u32[]{:S(2)}) collective-permute-start(bf16[128,1024]{1,0:T(8,128)(2,1)S(1)} %convolution_convert_fusion.2), channel_id=1, source_target_pairs={{32,0},{64,32},{96,64},{128,96},{160,128},{192,160},{224,192},{33,... | collective-permute-start | bytes 786440 | tf_op jit(solution)/shard_map/ppermute | solution.py:24
where the time goes:
time: 318 us; the launch traced here: 317 us
  blocking collectives  160 us (50%)
  waiting for transfers between devices  55.5 us (17%)
  matrix products  43.1 us (14%)
  other arithmetic  22.7 us (7%)
  starting transfers between devices  19.5 us (6%)
  local copies, waits for them, and re-layouts  15.2 us (5%)
    all_to_all x1, blocking collectives, in_one_piece(): lax.all_to_all(both, axis, split_axis=split_dim, concat_axis=concat_dim,...  160 us
    all_to_all x1, waiting for transfers between devices, body(): lax.all_to_all(input_grad, 'expert', split_axis=1, concat_axis=0, tiled=T...  55.5 us
    another operation x2, other arithmetic  18 us
    all_to_all x1, starting transfers between devices, body(): lax.all_to_all(input_grad, 'expert', split_axis=1, concat_axis=0, tiled=T...  9.68 us
    dot_general x1, matrix products, body(): jnp.einsum('tks,s->tk', select, back_routes.reshape(slot_total), preferre...  7.06 us
  transfers between devices with their start and end apart: 3, of which 1 were waited for; matrix products, arithmetic and copies ran while one was open for 10% of the time, Pallas kernels for 0%

commit v1 on v0

v1 whole, which is shorter than its diff:
```python
import functools

import jax
import jax.numpy as jnp
from jax import lax
from jax.experimental import pallas as pl
from jax.experimental.pallas import tpu as pltpu
from jax.sharding import PartitionSpec as P

NZ = 8
NX = 4
NS = 8
TOK = 128
TOPK = 8
D = 1024
H = 384
EL = 2
CAP = 24
ROW = EL * CAP
ER = EL * NX
ALL = NX * ROW
SRC = NX * CAP
MESH = pl.DeviceIdType.MESH
F32 = jnp.float32
BF16 = jnp.bfloat16


def dot(a, b):
    return jnp.dot(a, b, preferred_element_type=F32)


def dot_t(a, b):
    return lax.dot_general(a, b, (((1,), (1,)), ((), ())), preferred_element_type=F32)


def t_dot(a, b):
    return lax.dot_general(a, b, (((0,), (0,)), ((), ())), preferred_element_type=F32)


def iota(shape, dim):
    return lax.broadcasted_iota(jnp.int32, shape, dim)


def kernel(
    x_in, g_in, ids_in, lev_in, wg_in, wu_in, wd_in,
    up_out, rg_out, gate_out, upw_out, down_out,
    tok, meta, place, sel, got, wgu, wd, xs, ws, act, gug, ret, back, vret, vback,
    part, parts, gpart, gparts, upd, upd_d, ids_t, route_t,
    in_sem, ag_send, ag_recv, mt_send, mt_recv, s_send, s_recv, r_send, r_recv,
    v_send, v_recv, p_send, p_recv, g_send, g_recv, out_sem,
):
    s = lax.axis_index("section")
    e = lax.axis_index("expert")
    z = e // NX
    x = e % NX
    s_prev = (s + NS - 1) % NS
    s_next = (s + 1) % NS

    def device(section, zz, xx):
        return {"section": section, "expert": zz * NX + xx}

    def z_of(i):
        half = (i + 1) // 2
        return (z + NZ + half * (2 * (i % 2) - 1)) % NZ

    def z_from(i):
        half = (i + 1) // 2
        return (z + NZ - half * (2 * (i % 2) - 1)) % NZ

    def remote(src, dst, send, recv, to):
        return pltpu.make_async_remote_copy(
            src_ref=src, dst_ref=dst, send_sem=send, recv_sem=recv, device_id=to, device_id_type=MESH
        )

    own_in = pltpu.make_async_copy(x_in.at[0], tok.at[0, 0], in_sem.at[0])
    own_grad = pltpu.make_async_copy(g_in.at[0], tok.at[0, 1], in_sem.at[1])
    w_copies = [
        pltpu.make_async_copy(wg_in.at[0], wgu.at[:, :, pl.ds(0, H)], in_sem.at[2]),
        pltpu.make_async_copy(wu_in.at[0], wgu.at[:, :, pl.ds(H, H)], in_sem.at[3]),
        pltpu.make_async_copy(wd_in.at[0], wd, in_sem.at[4]),
    ]
    own_in.start()
    own_grad.start()

    barrier = pltpu.get_barrier_semaphore()

    def greet(to):
        pl.semaphore_signal(barrier, inc=1, device_id=to, device_id_type=MESH)

    for k in range(1, NZ):
        greet(device(s, (z + k) % NZ, x))
    for q in range(1, NX):
        greet(device(s, z, (x + q) % NX))
    for k in range(NZ):
        greet(device(s_prev, (z + k) % NZ, x))
        greet(device(s_next, (z + k) % NZ, x))
    for c in w_copies:
        c.start()

    eye = jnp.where(iota((TOK, TOK), 0) == iota((TOK, TOK), 1), 1.0, 0.0).astype(BF16)
    idt = t_dot(ids_in[0].astype(F32).astype(BF16), eye)
    rtt = t_dot(lev_in[0].astype(F32).astype(BF16), eye) / 256.0
    ids_t[...] = idt
    route_t[...] = rtt
    row = iota((TOK, TOK), 0)
    expert_of = ((row // 16) * 8 + row % 8).astype(F32)
    named = jnp.zeros((TOK, TOK), F32)
    route = jnp.zeros((TOK, TOK), F32)
    for k in range(TOPK):
        same = idt[k : k + 1, :] == expert_of
        named = jnp.where(same, 1.0, named)
        route = jnp.where(same, rtt[k : k + 1, :], route)
    before = jnp.where(iota((TOK, TOK), 0) < iota((TOK, TOK), 1), 1.0, 0.0).astype(BF16)
    slot = jnp.where(named > 0.5, dot(named.astype(BF16), before), -1.0)
    meta[0] = jnp.where(row % 16 < 8, slot, route).astype(BF16)

    own_in.wait()
    own_grad.wait()
    pl.semaphore_wait(barrier, (NZ - 1) + (NX - 1) + 2 * NZ)

    def ag(src, dst, h, to):
        return remote(tok.at[src, h], tok.at[dst, h], ag_send.at[dst, h], ag_recv.at[dst, h], to)

    def mt(src, dst, to):
        return remote(meta.at[src], meta.at[dst], mt_send.at[dst], mt_recv.at[dst], to)

    below = device(s, (z + NZ - 1) % NZ, x)
    above = device(s, (z + 1) % NZ, x)

    for h in range(2):
        ag(0, 1, h, below).start()
        ag(0, 2, h, above).start()
    mt(0, 1, below).start()
    mt(0, 2, above).start()

    def select(i):
        def forward():
            @pl.when(i < NZ)
            def _():
                mt(i, i, above).wait_recv()
                for h in range(2):
                    ag(i, i, h, above).wait_recv()

            to = device(s, (z + NZ + 1 - 2 * (i % 2)) % NZ, x)

            @pl.when(i < NZ - 3)
            def _():
                for h in range(2):
                    ag(i, i + 2, h, to).start()
                mt(i, i + 2, to).start()

            @pl.when(i == NZ - 3)
            def _():
                ag(NZ - 3, NZ - 1, 1, to).start()

            @pl.when(i == NZ - 2)
            def _():
                ag(NZ - 2, NZ - 1, 0, to).start()
                mt(NZ - 2, NZ - 1, to).start()

        pl.when(i > 0)(forward)

        group = meta[i, pl.ds(pl.multiple_of(z * 16, 16), 16), :].astype(F32)
        place_of = iota((CAP, TOK), 0).astype(F32)
        ones, routes = [], []
        for k in range(ER):
            hit = group[k : k + 1, :] == place_of
            ones.append(jnp.where(hit, 1.0, 0.0))
            routes.append(jnp.where(hit, group[ER + k : ER + k + 1, :], 0.0))
        one = jnp.concatenate(ones, axis=0).astype(BF16)
        weight = jnp.concatenate(routes, axis=0).astype(BF16)
        place[i] = one
        for h, chosen in ((0, one), (1, weight)):
            for n in range(0, D, 256):
                rows = dot(chosen, tok[i, h, :, n : n + 256]).astype(BF16)
                for q in range(NX):
                    sel[i, q, h, :, n : n + 256] = rows[q * ROW : (q + 1) * ROW]
        for q in range(1, NX):
            xx = (x + q) % NX
            sent(i, xx).start()
        got[i, x] = sel[i, x]

    def sent(i, xx):
        return remote(sel.at[i, xx], got.at[i, x], s_send.at[i, xx], s_recv.at[i, x], device(s, z, xx))

    def arrived(i, xx):
        return remote(sel.at[i, x], got.at[i, xx], s_send.at[i, xx], s_recv.at[i, xx], device(s, z, xx))

    def returned(i, xx):
        return remote(ret.at[i, xx], back.at[i, x], r_send.at[i, xx], r_recv.at[i, x], device(s, z, xx))

    def came_back(i, xx):
        return remote(ret.at[i, x], back.at[i, xx], r_send.at[i, xx], r_recv.at[i, xx], device(s, z, xx))

    def v_returned(i, xx):
        return remote(vret.at[i], vback.at[i, x], v_send.at[i, xx], v_recv.at[i, x], device(s, z, xx))

    def v_came_back(i, xx):
        return remote(vret.at[i], vback.at[i, xx], v_send.at[i, xx], v_recv.at[i, xx], device(s, z, xx))

    def expert_rows(i):
        for q in range(1, NX):
            arrived(i, (x + q) % NX).wait_recv()
        at = pl.ds(pl.multiple_of(i * SRC, 32), SRC)
        wide = [got[i, q, 0].astype(F32) for q in range(NX)]
        wide_w = [got[i, q, 1].astype(F32) for q in range(NX)]
        grads, vs = [], []
        for k in range(EL):
            mine = slice(k * CAP, (k + 1) * CAP)
            rows = jnp.concatenate([w[mine] for w in wide], axis=0).astype(BF16)
            weighted = jnp.concatenate([w[mine] for w in wide_w], axis=0).astype(BF16)
            xs[k, at, :] = rows
            ws[k, at, :] = weighted
            pre = dot(rows, wgu[k])
            gate, up = pre[:, :H], pre[:, H:]
            active_grad = dot_t(weighted, wd[k])
            sig = jax.nn.sigmoid(gate)
            silu = gate * sig
            active = (silu * up).astype(BF16)
            gate_grad = (active_grad * up * sig * (1.0 + gate * (1.0 - sig))).astype(BF16)
            up_grad = (active_grad * silu).astype(BF16)
            act[k, at, :] = active
            gug[k, at, 0:H] = gate_grad
            gug[k, at, H : 2 * H] = up_grad
            vs.append(jnp.sum(active.astype(F32) * active_grad, axis=1, keepdims=True))
            grads.append(jnp.concatenate([gate_grad, up_grad], axis=1))
        for n in range(0, D, 256):
            outs = [dot_t(grads[k], wgu[k, n : n + 256, :]) for k in range(EL)]
            for q in range(NX):
                piece = jnp.concatenate([o[q * CAP : (q + 1) * CAP] for o in outs], axis=0)
                ret[i, q, :, n : n + 256] = piece.astype(BF16)
        lines = []
        for q in range(NX):
            line = jnp.zeros((1, TOK), F32)
            for k in range(EL):
                at_lane = iota((CAP, TOK), 1) == iota((CAP, TOK), 0) + k * CAP
                line += jnp.sum(
                    jnp.where(at_lane, vs[k][q * CAP : (q + 1) * CAP], 0.0), axis=0, keepdims=True
                )
            lines.append(line)
        lines.append(jnp.zeros((8 - NX, TOK), F32))
        vret[i] = jnp.concatenate(lines, axis=0)
        for q in range(1, NX):
            xx = (x + q) % NX
            returned(i, xx).start()
            v_returned(i, xx).start()
        back[i, x] = ret[i, x]
        vback[i, x] = vret[i]

    def summed(i):
        return remote(part.at[i], parts.at[i], p_send.at[i], p_recv.at[i], device(s_prev, z_of(i), x))

    def g_summed(i):
        return remote(gpart.at[i], gparts.at[i], g_send.at[i], g_recv.at[i], device(s, z_of(i), x))

    def combine(i):
        for q in range(1, NX):
            came_back(i, (x + q) % NX).wait_recv()
            v_came_back(i, (x + q) % NX).wait_recv()
        one = place[i]
        for n in range(0, D, 256):
            rows = back[i, :, :, n : n + 256].reshape(ALL, 256)
            part[i, :, n : n + 256] = t_dot(one, rows).astype(BF16)
        summed(i).start()
        lines = []
        for q in range(NX):
            line = vback[i, q, pl.ds(x, 1), :]
            at_lane = iota((ROW, TOK), 1) == iota((ROW, TOK), 0)
            column = jnp.sum(jnp.where(at_lane, line, 0.0), axis=1, keepdims=True)
            spread = one[q * ROW : (q + 1) * ROW].astype(F32) * column
            for k in range(EL):
                lines.append(jnp.sum(spread[k * CAP : (k + 1) * CAP], axis=0, keepdims=True))
        gpart[i] = jnp.concatenate(lines, axis=0)

        @pl.when(i > 0)
        def _():
            g_summed(i).start()

        @pl.when(i == 0)
        def _():
            gparts[0] = gpart[0]

    def update(k):
        for m in range(0, D, 256):
            new = t_dot(xs[k, :, m : m + 256], gug[k])
            upd[k, 0, m : m + 256, :] = new[:, :H].astype(BF16)
            upd[k, 1, m : m + 256, :] = new[:, H:].astype(BF16)
        upd_d[k] = t_dot(act[k], ws[k]).astype(BF16)
        for c in outs_of(k):
            c.start()

    def outs_of(k):
        return [
            pltpu.make_async_copy(upd.at[k, 0], gate_out.at[0, k], out_sem.at[k, 0]),
            pltpu.make_async_copy(upd.at[k, 1], upw_out.at[0, k], out_sem.at[k, 1]),
            pltpu.make_async_copy(upd_d.at[k], down_out.at[0, k], out_sem.at[k, 2]),
        ]

    def step(t, carry):
        @pl.when(t < NZ)
        def _():
            select(t)

        @pl.when(t == 2)
        def _():
            for c in w_copies:
                c.wait()

        @pl.when(t >= 2)
        def _():
            expert_rows(t - 2)

        @pl.when(t >= 4)
        def _():
            combine(t - 4)

        return carry

    lax.fori_loop(0, NZ + 2, step, 0)
    combine(NZ - 2)
    update(0)
    combine(NZ - 1)
    update(1)

    for i in range(1, NZ):
        g_summed(i).wait_recv()
    acc = jnp.zeros((TOPK, TOK), F32)
    idt = ids_t[...]
    for i in range(NZ):
        base = z_from(i) * ER
        for k in range(ER):
            acc += jnp.where(idt == (base + k).astype(F32), gparts[i, k : k + 1, :], 0.0)
    final = (acc / route_t[...]).astype(BF16).astype(F32)
    square = jnp.concatenate([final, jnp.zeros((TOK - TOPK, TOK), F32)], axis=0).astype(BF16)
    rg_out[0] = dot_t(eye, square)[:, :TOPK].astype(BF16)

    total = None
    for i in range(NZ):
        summed(i).wait_recv()
        term = parts[i].astype(F32)
        total = term if total is None else total + term
    up_out[0] = jnp.where(s == NS - 1, 0.0, total).astype(BF16)

    def drain(i, carry):
        @pl.when(i > 0)
        def _():
            @pl.when(i < NZ)
            def _():
                mt(0, i, above).wait_send()
                for h in range(2):
                    ag(0, i, h, above).wait_send()

            g_summed(i).wait_send()

        for q in range(1, NX):
            xx = (x + q) % NX
            sent(i, xx).wait_send()
            returned(i, xx).wait_send()
            v_returned(i, xx).wait_send()
        summed(i).wait_send()
        return carry

    lax.fori_loop(0, NZ, drain, 0)
    for k in range(EL):
        for c in outs_of(k):
            c.wait()


def body(inputs, out_grads, expert_ids, route_levels, w_gate, w_up, w_down):
    any_spec = pl.BlockSpec(memory_space=pl.ANY)
    vmem = pl.BlockSpec(memory_space=pltpu.VMEM)
    dma = pltpu.SemaphoreType.DMA
    flops = 2 * 8 * EL * NZ * SRC * D * H
    return pl.pallas_call(
        kernel,
        name="layer_backward",
        out_shape=(
            jax.ShapeDtypeStruct((1, TOK, D), BF16),
            jax.ShapeDtypeStruct((1, TOK, TOPK), BF16),
            jax.ShapeDtypeStruct((1, EL, D, H), BF16),
            jax.ShapeDtypeStruct((1, EL, D, H), BF16),
            jax.ShapeDtypeStruct((1, EL, H, D), BF16),
        ),
        in_specs=[any_spec, any_spec, vmem, vmem, any_spec, any_spec, any_spec],
        out_specs=(vmem, vmem, any_spec, any_spec, any_spec),
        scratch_shapes=[
            pltpu.VMEM((NZ, 2, TOK, D), BF16),
            pltpu.VMEM((NZ, TOK, TOK), BF16),
            pltpu.VMEM((NZ, ALL, TOK), BF16),
            pltpu.VMEM((NZ, NX, 2, ROW, D), BF16),
            pltpu.VMEM((NZ, NX, 2, ROW, D), BF16),
            pltpu.VMEM((EL, D, 2 * H), BF16),
            pltpu.VMEM((EL, H, D), BF16),
            pltpu.VMEM((EL, NZ * SRC, D), BF16),
            pltpu.VMEM((EL, NZ * SRC, D), BF16),
            pltpu.VMEM((EL, NZ * SRC, H), BF16),
            pltpu.VMEM((EL, NZ * SRC, 2 * H), BF16),
            pltpu.VMEM((NZ, NX, ROW, D), BF16),
            pltpu.VMEM((NZ, NX, ROW, D), BF16),
            pltpu.VMEM((NZ, 8, TOK), F32),
            pltpu.VMEM((NZ, NX, 8, TOK), F32),
            pltpu.VMEM((NZ, TOK, D), BF16),
            pltpu.VMEM((NZ, TOK, D), BF16),
            pltpu.VMEM((NZ, ER, TOK), F32),
            pltpu.VMEM((NZ, ER, TOK), F32),
            pltpu.VMEM((EL, 2, D, H), BF16),
            pltpu.VMEM((EL, H, D), BF16),
            pltpu.VMEM((TOPK, TOK), F32),
            pltpu.VMEM((TOPK, TOK), F32),
            dma((5,)),
            dma((NZ, 2)),
            dma((NZ, 2)),
            dma((NZ,)),
            dma((NZ,)),
            dma((NZ, NX)),
            dma((NZ, NX)),
            dma((NZ, NX)),
            dma((NZ, NX)),
            dma((NZ, NX)),
            dma((NZ, NX)),
            dma((NZ,)),
            dma((NZ,)),
            dma((NZ,)),
            dma((NZ,)),
            dma((EL, 3)),
        ],
        compiler_params=pltpu.CompilerParams(
            collective_id=0, has_side_effects=True, vmem_limit_bytes=60 * 1024 * 1024
        ),
        cost_estimate=pl.CostEstimate(flops=flops, bytes_accessed=12 << 20, transcendentals=EL * NZ * SRC * H),
    )(inputs, out_grads, expert_ids, route_levels, w_gate, w_up, w_down)


def solution(mesh):
    rows = P("section", "expert", None)
    experts = P("section", "expert", None, None)
    return jax.shard_map(
        body,
        mesh=mesh,
        in_specs=(rows, rows, rows, rows, experts, experts, experts),
        out_specs=(rows, rows, experts, experts, experts),
        check_vma=False,
    )
```

time: 318 us -> 165 us (0.52)
  the two profiles are of different devices: /device:TPU:1 before, /device:TPU:97 now
where the time goes in v1:
time: 165 us; the launch traced here: 164 us
  Pallas kernels  152 us (92%)
  local copies, waits for them, and re-layouts  11.9 us (7%)
    pallas_call x1, Pallas kernels, body(): pl.pallas_call(kernel, name='layer_backward', out_shape=(jax.ShapeDtypeSt...  152 us
    unnamed x10, local copies, waits for them, and re-layouts  10.4 us

profile of v1, /device:TPU:97, one launch (start us, length us, event | category | flops | bytes accessed | tf_op | source)
XLA Modules:
  0.0 164.2 jit_solution(4165022946462537599)
XLA Ops:
  0.6 1.4 copy.12.ids_in
  2.0 1.4 copy.13.lev_in
  3.5 151.7 %layer_backward.1 = (bf16[1,128,1024]{2,1,0:T(8,128)(2,1)}, bf16[1,128,8]{2,1,0:T(8,128)(2,1)}, bf16[1,2,1024,384]{3,2,1,0:T(8,128)(2,1)}, bf16[1,2,1024,384]{3,2,1,0:T(8,128)(2,1)}, bf16[1,2,384,1024]{3,2,1,0:T(8,128)(2,1)}) custom-call(bf16[1,128,1024]{2,1,0:T(8,128)(2,1)} %x_in.1, bf16[1,128,1024]{2,1,0:T(8,128)(2,1)} %g_in.1, s32[1,128,8]{2,1,0:T(8,128)} %copy.12.ids_in, ...), custom_call_target="tpu_custom_call" | custom-call | flops 9663676416 | bytes 12582912 | tf_op jit(solution)/shard_map/layer_backward/pallas_call | solution.py:374
  155.2 1.4 copy.14
  156.6 1.7 %copy.19 = bf16[1,128,1024]{2,1,0:T(8,128)(2,1)} copy(bf16[1,128,1024]{2,1,0:T(8,128)(2,1)} %get-tuple-element.15) | data formatting | bytes 524288
  158.2 0.0 copy-start.1
  158.3 2.8 %copy.20 = bf16[1,2,1024,384]{3,2,1,0:T(8,128)(2,1)} copy(bf16[1,2,1024,384]{3,2,1,0:T(8,128)(2,1)} %get-tuple-element.17) | data formatting | bytes 3145728
  161.1 0.0 copy-done.1
  161.1 0.0 copy-start
  161.1 1.1 copy.21
  162.2 0.8 copy-done
  163.1 1.1 copy.22
Async XLA Ops:
  158.2 2.8 %copy-start.1 = (bf16[1,2,1024,384]{3,2,1,0:T(8,128)(2,1)S(1)}, bf16[1,2,1024,384]{3,2,1,0:T(8,128)(2,1)}, u32[]{:S(2)}) copy-start(bf16[1,2,1024,384]{3,2,1,0:T(8,128)(2,1)} %get-tuple-element.18) | copy-start | bytes 4718596
  161.1 2.0 %copy-start = (bf16[1,2,384,1024]{3,2,1,0:T(8,128)(2,1)S(1)}, bf16[1,2,384,1024]{3,2,1,0:T(8,128)(2,1)}, u32[]{:S(2)}) copy-start(bf16[1,2,384,1024]{3,2,1,0:T(8,128)(2,1)} %get-tuple-element.19) | copy-start | bytes 4718596

commit v2 on v1

v2 whole, which is shorter than its diff:
```python
import jax
import jax.numpy as jnp
from jax import lax
from jax.experimental import pallas as pl
from jax.experimental.pallas import tpu as pltpu
from jax.sharding import PartitionSpec as P

NZ = 8
NX = 4
NS = 8
TOK = 128
TOPK = 8
D = 1024
H = 384
EL = 2
CAP = 24
ROW = EL * CAP
ER = EL * NX
ALL = NX * ROW
SRC = NX * CAP
AWAY = (0, 1, -1, 2, -2, 3, -3, 4)
MESH = pl.DeviceIdType.MESH
F32 = jnp.float32
BF16 = jnp.bfloat16


def dot(a, b):
    return jnp.dot(a, b, preferred_element_type=F32)


def dot_t(a, b):
    return lax.dot_general(a, b, (((1,), (1,)), ((), ())), preferred_element_type=F32)


def t_dot(a, b):
    return lax.dot_general(a, b, (((0,), (0,)), ((), ())), preferred_element_type=F32)


def iota(shape, dim):
    return lax.broadcasted_iota(jnp.int32, shape, dim)


def kernel(
    x_in, g_in, ids_in, lev_in, wg_in, wu_in, wd_in,
    up_out, rg_out, gate_out, upw_out, down_out,
    tok, meta, place, place_w, sel, got, wgu, wd, xs, ws, act, gug, ret, back, vret, vback,
    part, inc, fin, gpart, gparts, upd, upd_d,
    in_sem, ag_send, ag_recv, mt_send, mt_recv, s_send, s_recv, r_send, r_recv,
    v_send, v_recv, p_send, p_recv, f_send, f_recv, g_send, g_recv, out_sem,
):
    s = lax.axis_index("section")
    e = lax.axis_index("expert")
    z = e // NX
    x = e % NX
    s_prev = (s + NS - 1) % NS
    s_next = (s + 1) % NS
    others = [(x + q) % NX for q in range(1, NX)]

    def device(section, zz, xx):
        return {"section": section, "expert": ((zz + NZ) % NZ) * NX + xx}

    below, above = device(s, z - 1, x), device(s, z + 1, x)

    def remote(src, dst, send, recv, to):
        return pltpu.make_async_remote_copy(
            src_ref=src, dst_ref=dst, send_sem=send, recv_sem=recv, device_id=to, device_id_type=MESH
        )

    def ag(src, dst, h, to):
        return remote(tok.at[src, h], tok.at[dst, h], ag_send.at[dst, h], ag_recv.at[dst, h], to)

    def mt(src, dst, to):
        return remote(meta.at[src], meta.at[dst], mt_send.at[dst], mt_recv.at[dst], to)

    def sent(i, h, xx):
        return remote(
            sel.at[i, xx, h], got.at[i, x, h], s_send.at[i, xx, h], s_recv.at[i, x, h], device(s, z, xx)
        )

    def arrived(i, h, xx):
        return remote(
            sel.at[i, x, h], got.at[i, xx, h], s_send.at[i, xx, h], s_recv.at[i, xx, h], device(s, z, xx)
        )

    def returned(i, xx):
        return remote(ret.at[i, xx], back.at[i, x], r_send.at[i, xx], r_recv.at[i, x], device(s, z, xx))

    def came_back(i, xx):
        return remote(ret.at[i, x], back.at[i, xx], r_send.at[i, xx], r_recv.at[i, xx], device(s, z, xx))

    def v_returned(i, xx):
        return remote(vret.at[i], vback.at[i, x], v_send.at[i, xx], v_recv.at[i, x], device(s, z, xx))

    def v_came_back(i, xx):
        return remote(vret.at[i], vback.at[i, xx], v_send.at[i, xx], v_recv.at[i, xx], device(s, z, xx))

    def onward(i):
        if i == 7:
            low, high = pl.ds(0, D // 2), pl.ds(D // 2, D // 2)
            return [
                remote(part.at[7, :, low], inc.at[5, :, low], p_send.at[5], p_recv.at[5], above),
                remote(part.at[7, :, high], inc.at[6, :, high], p_send.at[6], p_recv.at[6], below),
            ]
        if i > 2:
            to = above if i % 2 else below
            return [remote(part.at[i], inc.at[i - 2], p_send.at[i - 2], p_recv.at[i - 2], to)]
        to = device(s_prev, z + AWAY[i], x)
        return [remote(part.at[i], fin.at[i], f_send.at[i], f_recv.at[i], to)]

    def incoming(i):
        return onward(7)[i - 5] if i > 4 else onward(i + 2)[0]

    def g_summed(i):
        return remote(gpart.at[i], gparts.at[i], g_send.at[i], g_recv.at[i], device(s, z + AWAY[i], x))

    own_in = pltpu.make_async_copy(x_in.at[0], tok.at[0, 0], in_sem.at[0])
    own_grad = pltpu.make_async_copy(g_in.at[0], tok.at[0, 1], in_sem.at[1])
    w_copies = [
        pltpu.make_async_copy(wg_in.at[0], wgu.at[:, :, pl.ds(0, H)], in_sem.at[2]),
        pltpu.make_async_copy(wu_in.at[0], wgu.at[:, :, pl.ds(H, H)], in_sem.at[3]),
        pltpu.make_async_copy(wd_in.at[0], wd, in_sem.at[4]),
    ]
    own_in.start()
    own_grad.start()

    barrier = pltpu.get_barrier_semaphore()

    def greet(to):
        pl.semaphore_signal(barrier, inc=1, device_id=to, device_id_type=MESH)

    for k in range(1, NZ):
        greet(device(s, z + k, x))
    for xx in others:
        greet(device(s, z, xx))
    for k in (-1, 0, 1):
        greet(device(s_prev, z + k, x))
        greet(device(s_next, z + k, x))
    for c in w_copies:
        c.start()

    idt = ids_in[0].astype(F32)
    rtt = lev_in[0].astype(F32) / 256.0
    row = iota((TOK, TOK), 0)
    expert_of = ((row // 16) * 8 + row % 8).astype(F32)
    named = jnp.zeros((TOK, TOK), F32)
    route = jnp.zeros((TOK, TOK), F32)
    for k in range(TOPK):
        same = idt[k : k + 1, :] == expert_of
        named = jnp.where(same, 1.0, named)
        route = jnp.where(same, rtt[k : k + 1, :], route)
    before = jnp.where(iota((TOK, TOK), 0) < iota((TOK, TOK), 1), 1.0, 0.0).astype(BF16)
    slot = jnp.where(named > 0.5, dot(named.astype(BF16), before), -1.0)
    meta[0] = jnp.where(row % 16 < 8, slot, route).astype(BF16)

    def places(i):
        group = meta[i, pl.ds(pl.multiple_of(z * 16, 16), 16), :].astype(F32)
        place_of = iota((CAP, TOK), 0).astype(F32)
        ones, routes = [], []
        for k in range(ER):
            hit = group[k : k + 1, :] == place_of
            ones.append(jnp.where(hit, 1.0, 0.0))
            routes.append(jnp.where(hit, group[ER + k : ER + k + 1, :], 0.0))
        place[i] = jnp.concatenate(ones, axis=0).astype(BF16)
        place_w[i] = jnp.concatenate(routes, axis=0).astype(BF16)

    def chosen(i, h):
        if h == 0:
            places(i)
        which = place_w[i] if h else place[i]
        for n in range(0, D, 256):
            rows = dot(which, tok[i, h, :, n : n + 256]).astype(BF16)
            for q in range(NX):
                sel[i, q, h, :, n : n + 256] = rows[q * ROW : (q + 1) * ROW]

    def send_chosen(i, h):
        for xx in others:
            sent(i, h, xx).start()
        got[i, x, h] = sel[i, x, h]

    def pass_on(i, h):
        if h == 0:
            mt(i, i, above).wait_recv()
        ag(i, i, h, above).wait_recv()
        if i == 7 or (i == 5 and h == 0) or (i == 6 and h == 1):
            return
        to, dst = (below, above)[1 - i % 2], min(i + 2, 7)
        if h == 0:
            mt(i, dst, to).start()
        ag(i, dst, h, to).start()

    def select(i, h):
        chosen(i, h)
        send_chosen(i, h)

    def expert_rows(i):
        for xx in others:
            for h in range(2):
                arrived(i, h, xx).wait_recv()
        at = slice(i * SRC, (i + 1) * SRC)
        wide = [got[i, q, 0].astype(F32) for q in range(NX)]
        wide_w = [got[i, q, 1].astype(F32) for q in range(NX)]
        grads, vs = [], []
        for k in range(EL):
            mine = slice(k * CAP, (k + 1) * CAP)
            rows = jnp.concatenate([w[mine] for w in wide], axis=0).astype(BF16)
            weighted = jnp.concatenate([w[mine] for w in wide_w], axis=0).astype(BF16)
            xs[k, at, :] = rows
            ws[k, at, :] = weighted
            pre = dot(rows, wgu[k])
            gate, up = pre[:, :H], pre[:, H:]
            active_grad = dot_t(weighted, wd[k])
            sig = jax.nn.sigmoid(gate)
            silu = gate * sig
            active = (silu * up).astype(BF16)
            gate_grad = (active_grad * up * sig * (1.0 + gate * (1.0 - sig))).astype(BF16)
            up_grad = (active_grad * silu).astype(BF16)
            act[k, at, :] = active
            gug[k, at, 0:H] = gate_grad
            gug[k, at, H : 2 * H] = up_grad
            vs.append(jnp.sum(active.astype(F32) * active_grad, axis=1, keepdims=True))
            grads.append(jnp.concatenate([gate_grad, up_grad], axis=1))
        for n in range(0, D, 256):
            outs = [dot_t(grads[k], wgu[k, n : n + 256, :]) for k in range(EL)]
            for q in range(NX):
                piece = jnp.concatenate([o[q * CAP : (q + 1) * CAP] for o in outs], axis=0)
                ret[i, q, :, n : n + 256] = piece.astype(BF16)
        lines = []
        for q in range(NX):
            line = jnp.zeros((1, TOK), F32)
            for k in range(EL):
                at_lane = iota((CAP, TOK), 1) == iota((CAP, TOK), 0) + k * CAP
                line += jnp.sum(
                    jnp.where(at_lane, vs[k][q * CAP : (q + 1) * CAP], 0.0), axis=0, keepdims=True
                )
            lines.append(line)
        lines.append(jnp.zeros((8 - NX, TOK), F32))
        vret[i] = jnp.concatenate(lines, axis=0)
        back[i, x] = ret[i, x]
        vback[i, x] = vret[i]

    def send_back(i):
        for xx in others:
            returned(i, xx).start()
            v_returned(i, xx).start()

    def combine(i):
        for xx in others:
            came_back(i, xx).wait_recv()
            v_came_back(i, xx).wait_recv()
        if 0 < i < 7:
            incoming(i).wait_recv()
        one = place[i]
        for n in range(0, D, 256):
            rows = back[i, :, :, n : n + 256].reshape(ALL, 256)
            total = t_dot(one, rows)
            if 0 < i < 5 or (i == 5 and n < D // 2) or (i == 6 and n >= D // 2):
                total += inc[i, :, n : n + 256].astype(F32)
            part[i, :, n : n + 256] = total.astype(BF16)
        for c in onward(i):
            c.start()
        lines = []
        for q in range(NX):
            line = vback[i, q, pl.ds(x, 1), :]
            at_lane = iota((ROW, TOK), 1) == iota((ROW, TOK), 0)
            column = jnp.sum(jnp.where(at_lane, line, 0.0), axis=1, keepdims=True)
            spread = one[q * ROW : (q + 1) * ROW].astype(F32) * column
            for k in range(EL):
                lines.append(jnp.sum(spread[k * CAP : (k + 1) * CAP], axis=0, keepdims=True))
        summed = jnp.concatenate(lines, axis=0)
        if i:
            gpart[i] = summed
            g_summed(i).start()
        else:
            gparts[0] = summed

    def outs_of(k):
        return [
            pltpu.make_async_copy(upd.at[k, 0], gate_out.at[0, k], out_sem.at[k, 0]),
            pltpu.make_async_copy(upd.at[k, 1], upw_out.at[0, k], out_sem.at[k, 1]),
            pltpu.make_async_copy(upd_d.at[k], down_out.at[0, k], out_sem.at[k, 2]),
        ]

    def update(k, stage):
        if stage < 2:
            for m in range(stage * D // 2, (stage + 1) * D // 2, 256):
                new = t_dot(xs[k, :, m : m + 256], gug[k])
                upd[k, 0, m : m + 256, :] = new[:, :H].astype(BF16)
                upd[k, 1, m : m + 256, :] = new[:, H:].astype(BF16)
        else:
            upd_d[k] = t_dot(act[k], ws[k]).astype(BF16)
            for c in outs_of(k):
                c.start()

    own_in.wait()
    own_grad.wait()
    chosen(0, 0)
    chosen(0, 1)
    pl.semaphore_wait(barrier, (NZ - 1) + (NX - 1) + 6)
    mt(0, 1, below).start()
    mt(0, 2, above).start()
    for h in range(2):
        ag(0, 1, h, below).start()
        ag(0, 2, h, above).start()
        send_chosen(0, h)

    def both(a, b, h):
        pass_on(a, h)
        pass_on(b, h)
        select(a, h)
        select(b, h)

    both(1, 2, 0)
    both(1, 2, 1)
    for c in w_copies:
        c.wait()
    expert_rows(0)
    both(3, 4, 0)
    expert_rows(1)
    both(3, 4, 1)
    expert_rows(2)
    both(5, 6, 0)
    expert_rows(3)
    pass_on(5, 1)
    pass_on(6, 1)
    select(5, 1)
    pass_on(7, 0)
    pass_on(7, 1)
    select(7, 0)
    select(7, 1)
    select(6, 1)
    expert_rows(4)
    expert_rows(5)
    expert_rows(7)
    send_back(7)
    send_back(5)
    expert_rows(6)
    for i in (6, 3, 4, 1, 2, 0):
        send_back(i)
    combine(7)
    update(0, 0)
    combine(5)
    update(0, 1)
    combine(6)
    update(0, 2)
    combine(3)
    update(1, 0)
    combine(4)
    update(1, 1)
    combine(1)
    update(1, 2)
    combine(2)
    combine(0)

    for i in range(1, NZ):
        g_summed(i).wait_recv()
    acc = jnp.zeros((TOPK, TOK), F32)
    idt = ids_in[0].astype(F32)
    for i in range(NZ):
        base = ((z + NZ - AWAY[i]) % NZ) * ER
        for k in range(ER):
            acc += jnp.where(idt == (base + k).astype(F32), gparts[i, k : k + 1, :], 0.0)
    rg_out[0] = (acc / (lev_in[0].astype(F32) / 256.0)).astype(BF16)

    for i in range(3):
        onward(i)[0].wait_recv()
    total = fin[0].astype(F32) + fin[1].astype(F32) + fin[2].astype(F32)
    up_out[0] = jnp.where(s == NS - 1, 0.0, total).astype(BF16)

    for i in range(NZ):
        if i:
            mt(0, i, above).wait_send()
            for h in range(2):
                ag(0, i, h, above).wait_send()
            g_summed(i).wait_send()
        for xx in others:
            for h in range(2):
                sent(i, h, xx).wait_send()
            returned(i, xx).wait_send()
            v_returned(i, xx).wait_send()
        for c in onward(i):
            c.wait_send()
    for k in range(EL):
        for c in outs_of(k):
            c.wait()


def body(inputs, out_grads, expert_ids, route_levels, w_gate, w_up, w_down):
    any_spec = pl.BlockSpec(memory_space=pl.ANY)
    vmem = pl.BlockSpec(memory_space=pltpu.VMEM)
    dma = pltpu.SemaphoreType.DMA
    flops = 2 * 8 * EL * NZ * SRC * D * H
    upstream, route_grad, *updates = pl.pallas_call(
        kernel,
        name="layer_backward",
        out_shape=(
            jax.ShapeDtypeStruct((1, TOK, D), BF16),
            jax.ShapeDtypeStruct((1, TOPK, TOK), BF16),
            jax.ShapeDtypeStruct((1, EL, D, H), BF16),
            jax.ShapeDtypeStruct((1, EL, D, H), BF16),
            jax.ShapeDtypeStruct((1, EL, H, D), BF16),
        ),
        in_specs=[any_spec, any_spec, vmem, vmem, any_spec, any_spec, any_spec],
        out_specs=(vmem, vmem, any_spec, any_spec, any_spec),
        scratch_shapes=[
            pltpu.VMEM((NZ, 2, TOK, D), BF16),
            pltpu.VMEM((NZ, TOK, TOK), BF16),
            pltpu.VMEM((NZ, ALL, TOK), BF16),
            pltpu.VMEM((NZ, ALL, TOK), BF16),
            pltpu.VMEM((NZ, NX, 2, ROW, D), BF16),
            pltpu.VMEM((NZ, NX, 2, ROW, D), BF16),
            pltpu.VMEM((EL, D, 2 * H), BF16),
            pltpu.VMEM((EL, H, D), BF16),
            pltpu.VMEM((EL, NZ * SRC, D), BF16),
            pltpu.VMEM((EL, NZ * SRC, D), BF16),
            pltpu.VMEM((EL, NZ * SRC, H), BF16),
            pltpu.VMEM((EL, NZ * SRC, 2 * H), BF16),
            pltpu.VMEM((NZ, NX, ROW, D), BF16),
            pltpu.VMEM((NZ, NX, ROW, D), BF16),
            pltpu.VMEM((NZ, 8, TOK), F32),
            pltpu.VMEM((NZ, NX, 8, TOK), F32),
            pltpu.VMEM((NZ, TOK, D), BF16),
            pltpu.VMEM((NZ, TOK, D), BF16),
            pltpu.VMEM((3, TOK, D), BF16),
            pltpu.VMEM((NZ, ER, TOK), F32),
            pltpu.VMEM((NZ, ER, TOK), F32),
            pltpu.VMEM((EL, 2, D, H), BF16),
            pltpu.VMEM((EL, H, D), BF16),
            dma((5,)),
            dma((NZ, 2)),
            dma((NZ, 2)),
            dma((NZ,)),
            dma((NZ,)),
            dma((NZ, NX, 2)),
            dma((NZ, NX, 2)),
            dma((NZ, NX)),
            dma((NZ, NX)),
            dma((NZ, NX)),
            dma((NZ, NX)),
            dma((NZ,)),
            dma((NZ,)),
            dma((3,)),
            dma((3,)),
            dma((NZ,)),
            dma((NZ,)),
            dma((EL, 3)),
        ],
        compiler_params=pltpu.CompilerParams(
            collective_id=0, has_side_effects=True, vmem_limit_bytes=60 * 1024 * 1024
        ),
        cost_estimate=pl.CostEstimate(flops=flops, bytes_accessed=12 << 20, transcendentals=EL * NZ * SRC * H),
    )(inputs, out_grads, jnp.swapaxes(expert_ids, 1, 2), jnp.swapaxes(route_levels, 1, 2), w_gate, w_up, w_down)
    return (upstream, jnp.swapaxes(route_grad, 1, 2), *updates)


def solution(mesh):
    rows = P("section", "expert", None)
    experts = P("section", "expert", None, None)
    return jax.shard_map(
        body,
        mesh=mesh,
        in_specs=(rows, rows, rows, rows, experts, experts, experts),
        out_specs=(rows, rows, experts, experts, experts),
        check_vma=False,
    )
```

time: 165 us -> 137 us (0.83)
  the two profiles are of different devices: /device:TPU:97 before, /device:TPU:1 now
where the time goes in v2:
time: 137 us
  Pallas kernels  127 us (93%)
  local copies, waits for them, and re-layouts  8.87 us (6%)
    pallas_call x1, Pallas kernels, body(): pl.pallas_call(kernel, name='layer_backward', out_shape=(jax.ShapeDtypeSt...  127 us
    unnamed x9, local copies, waits for them, and re-layouts  8.87 us

profile of v2, /device:TPU:1, one launch (start us, length us, event | category | flops | bytes accessed | tf_op | source)
XLA Modules:
  0.0 136.7 jit_solution(7249305704192787560)
XLA Ops:
  0.6 127.2 %layer_backward.1 = (bf16[1,128,1024]{2,1,0:T(8,128)(2,1)}, bf16[1,8,128]{2,1,0:T(8,128)(2,1)}, bf16[1,2,1024,384]{3,2,1,0:T(8,128)(2,1)}, bf16[1,2,1024,384]{3,2,1,0:T(8,128)(2,1)}, bf16[1,2,384,1024]{3,2,1,0:T(8,128)(2,1)}) custom-call(bf16[1,128,1024]{2,1,0:T(8,128)(2,1)} %x_in.1, bf16[1,128,1024]{2,1,0:T(8,128)(2,1)} %g_in.1, s32[1,8,128]{2,1,0:T(8,128)} %bitcast.4, ...), custom_call_target="tpu_custom_call" | custom-call | flops 9663676416 | bytes 12582912 | tf_op jit(solution)/shard_map/layer_backward/pallas_call | solution.py:392
  127.8 1.7 %copy.17 = bf16[1,128,1024]{2,1,0:T(8,128)(2,1)} copy(bf16[1,128,1024]{2,1,0:T(8,128)(2,1)} %get-tuple-element.20) | data formatting | bytes 524288
  129.5 1.3 copy.18
  130.8 0.0 copy-start.1
  130.8 2.8 %copy.19 = bf16[1,2,1024,384]{3,2,1,0:T(8,128)(2,1)} copy(bf16[1,2,1024,384]{3,2,1,0:T(8,128)(2,1)} %get-tuple-element.22) | data formatting | bytes 3145728
  133.6 0.0 copy-done.1
  133.6 0.0 copy-start
  133.6 1.1 copy.20
  134.7 0.8 copy-done
  135.6 1.1 copy.21
Async XLA Ops:
  130.8 2.8 %copy-start.1 = (bf16[1,2,1024,384]{3,2,1,0:T(8,128)(2,1)S(1)}, bf16[1,2,1024,384]{3,2,1,0:T(8,128)(2,1)}, u32[]{:S(2)}) copy-start(bf16[1,2,1024,384]{3,2,1,0:T(8,128)(2,1)} %get-tuple-element.23) | copy-start | bytes 4718596
  133.6 2.0 %copy-start = (bf16[1,2,384,1024]{3,2,1,0:T(8,128)(2,1)S(1)}, bf16[1,2,384,1024]{3,2,1,0:T(8,128)(2,1)}, u32[]{:S(2)}) copy-start(bf16[1,2,384,1024]{3,2,1,0:T(8,128)(2,1)} %get-tuple-element.24) | copy-start | bytes 4718596

commit v3 on v2

--- a/solution.py
+++ b/solution.py
@@ -44,9 +44,9 @@
     x_in, g_in, ids_in, lev_in, wg_in, wu_in, wd_in,
     up_out, rg_out, gate_out, upw_out, down_out,
     tok, meta, place, place_w, sel, got, wgu, wd, xs, ws, act, gug, ret, back, vret, vback,
-    part, inc, fin, gpart, gparts, upd, upd_d,
+    part, inc, fin, gpart, gparts,
     in_sem, ag_send, ag_recv, mt_send, mt_recv, s_send, s_recv, r_send, r_recv,
-    v_send, v_recv, p_send, p_recv, f_send, f_recv, g_send, g_recv, out_sem,
+    v_send, v_recv, p_send, p_recv, f_send, f_recv, g_send, g_recv,
 ):
     s = lax.axis_index("section")
     e = lax.axis_index("expert")
@@ -273,23 +273,14 @@
         else:
             gparts[0] = summed
 
-    def outs_of(k):
-        return [
-            pltpu.make_async_copy(upd.at[k, 0], gate_out.at[0, k], out_sem.at[k, 0]),
-            pltpu.make_async_copy(upd.at[k, 1], upw_out.at[0, k], out_sem.at[k, 1]),
-            pltpu.make_async_copy(upd_d.at[k], down_out.at[0, k], out_sem.at[k, 2]),
-        ]
-
     def update(k, stage):
         if stage < 2:
             for m in range(stage * D // 2, (stage + 1) * D // 2, 256):
                 new = t_dot(xs[k, :, m : m + 256], gug[k])
-                upd[k, 0, m : m + 256, :] = new[:, :H].astype(BF16)
-                upd[k, 1, m : m + 256, :] = new[:, H:].astype(BF16)
+                gate_out[0, k, m : m + 256, :] = new[:, :H].astype(BF16)
+                upw_out[0, k, m : m + 256, :] = new[:, H:].astype(BF16)
         else:
-            upd_d[k] = t_dot(act[k], ws[k]).astype(BF16)
-            for c in outs_of(k):
-                c.start()
+            down_out[0, k] = t_dot(act[k], ws[k]).astype(BF16)
 
     own_in.wait()
     own_grad.wait()
@@ -379,9 +370,15 @@
             v_returned(i, xx).wait_send()
         for c in onward(i):
             c.wait_send()
-    for k in range(EL):
-        for c in outs_of(k):
-            c.wait()
+
+
+def write_out(*refs):
+    count = (len(refs) - 1) // 2
+    copies = [pltpu.make_async_copy(refs[k], refs[count + k], refs[-1].at[k]) for k in range(count)]
+    for c in copies:
+        c.start()
+    for c in copies:
+        c.wait()
 
 
 def body(inputs, out_grads, expert_ids, route_levels, w_gate, w_up, w_down):
@@ -389,18 +386,13 @@
     vmem = pl.BlockSpec(memory_space=pltpu.VMEM)
     dma = pltpu.SemaphoreType.DMA
     flops = 2 * 8 * EL * NZ * SRC * D * H
-    upstream, route_grad, *updates = pl.pallas_call(
+    shapes = [(1, TOK, D), (1, TOPK, TOK), (1, EL, D, H), (1, EL, D, H), (1, EL, H, D)]
+    results = pl.pallas_call(
         kernel,
         name="layer_backward",
-        out_shape=(
-            jax.ShapeDtypeStruct((1, TOK, D), BF16),
-            jax.ShapeDtypeStruct((1, TOPK, TOK), BF16),
-            jax.ShapeDtypeStruct((1, EL, D, H), BF16),
-            jax.ShapeDtypeStruct((1, EL, D, H), BF16),
-            jax.ShapeDtypeStruct((1, EL, H, D), BF16),
-        ),
+        out_shape=[pltpu.VMEM(shape, BF16) for shape in shapes],
         in_specs=[any_spec, any_spec, vmem, vmem, any_spec, any_spec, any_spec],
-        out_specs=(vmem, vmem, any_spec, any_spec, any_spec),
+        out_specs=[vmem] * 5,
         scratch_shapes=[
             pltpu.VMEM((NZ, 2, TOK, D), BF16),
             pltpu.VMEM((NZ, TOK, TOK), BF16),
@@ -423,8 +415,6 @@
             pltpu.VMEM((3, TOK, D), BF16),
             pltpu.VMEM((NZ, ER, TOK), F32),
             pltpu.VMEM((NZ, ER, TOK), F32),
-            pltpu.VMEM((EL, 2, D, H), BF16),
-            pltpu.VMEM((EL, H, D), BF16),
             dma((5,)),
             dma((NZ, 2)),
             dma((NZ, 2)),
@@ -442,13 +432,22 @@
             dma((3,)),
             dma((NZ,)),
             dma((NZ,)),
-            dma((EL, 3)),
         ],
         compiler_params=pltpu.CompilerParams(
-            collective_id=0, has_side_effects=True, vmem_limit_bytes=60 * 1024 * 1024
+            collective_id=0, has_side_effects=True, vmem_limit_bytes=56 * 1024 * 1024
         ),
         cost_estimate=pl.CostEstimate(flops=flops, bytes_accessed=12 << 20, transcendentals=EL * NZ * SRC * H),
     )(inputs, out_grads, jnp.swapaxes(expert_ids, 1, 2), jnp.swapaxes(route_levels, 1, 2), w_gate, w_up, w_down)
+    upstream, route_grad, *updates = pl.pallas_call(
+        write_out,
+        name="write_out",
+        out_shape=[jax.ShapeDtypeStruct(shape, BF16) for shape in shapes],
+        in_specs=[any_spec] * 5,
+        out_specs=[any_spec] * 5,
+        scratch_shapes=[dma((5,))],
+        compiler_params=pltpu.CompilerParams(vmem_limit_bytes=1 << 20),
+        cost_estimate=pl.CostEstimate(flops=0, bytes_accessed=5 << 20, transcendentals=0),
+    )(*results)
     return (upstream, jnp.swapaxes(route_grad, 1, 2), *updates)
 
 

time: 137 us -> 130 us (0.949)
  local copies, waits for them, and re-layouts: 8.87 us -> 0 us
  Pallas kernels: 127 us -> 129 us
    unnamed x9 -> x0, local copies, waits for them, and re-layouts: 8.87 us -> none
    pallas_call x1 -> x2, Pallas kernels: 127 us -> 129 us  [the longest x1 126 us: body(): pl.pallas_call(kernel, name='layer_backward', out_shape=[pltpu.VMEM(shape...]
where the time goes in v3:
time: 130 us
  Pallas kernels  129 us (99%)
    pallas_call x1, Pallas kernels, body(): pl.pallas_call(kernel, name='layer_backward', out_shape=[pltpu.VMEM(shape...  126 us

profile of v3, /device:TPU:1, one launch (start us, length us, event | category | flops | bytes accessed | tf_op | source)
XLA Modules:
  0.0 129.6 jit_solution(14700575874039993694)
XLA Ops:
  0.6 126.4 %layer_backward.1 = (bf16[1,128,1024]{2,1,0:T(8,128)(2,1)S(1)}, bf16[1,8,128]{2,1,0:T(8,128)(2,1)S(1)}, bf16[1,2,1024,384]{3,2,1,0:T(8,128)(2,1)S(1)}, bf16[1,2,...) custom-call(bf16[1,128,1024]{2,1,0:T(8,128)(2,1)} %x_in.1, bf16[1,128,1024]{2,1,0:T(8,128)(2,1)} %g_in.1, ...), custom_call_target="tpu_custom_call" | custom-call | flops 9663676416 | bytes 12582912 | tf_op jit(solution)/shard_map/layer_backward/pallas_call | solution.py:390
  127.1 2.3 %write_out.1 = (bf16[1,128,1024]{2,1,0:T(8,128)(2,1)}, bf16[1,8,128]{2,1,0:T(8,128)(2,1)}, bf16[1,2,1024,384]{3,2,1,0:T(8,128)(2,1)}, bf16[1,2,1024,384]{3,2,1,0:T(8,128)(2,1)}, bf16[1,2,384,1024]{3,2,1,0:T(8,128)(2,1)}) custom-call(bf16[1,128,1024]{2,1,0:T(8,128)(2,1)S(1)} %get-tuple-element.15.refs_0_, bf16[1,8,128]{2,1,0:T(8,128)(2,1)S(1)} %get-tuple-element.16.refs_1_, ...), custom_call_target="tpu_custom_call" | custom-call | bytes 5242880 | tf_op jit(solution)/shard_map/write_out/pallas_call | solution.py:441

commit v4 on v3

--- a/solution.py
+++ b/solution.py
@@ -11,6 +11,8 @@
 TOK = 128
 TOPK = 8
 D = 1024
+CW = 256
+DA = D - CW
 H = 384
 EL = 2
 CAP = 24
@@ -43,9 +45,9 @@
 def kernel(
     x_in, g_in, ids_in, lev_in, wg_in, wu_in, wd_in,
     up_out, rg_out, gate_out, upw_out, down_out,
-    tok, meta, place, place_w, sel, got, wgu, wd, xs, ws, act, gug, ret, back, vret, vback,
+    tok, meta, cx, mo, mx, mf, zs, gotc, place, place_w, sel, got, wgu, wd, xs, ws, act, gug, ret, back, vret, vback,
     part, inc, fin, gpart, gparts,
-    in_sem, ag_send, ag_recv, mt_send, mt_recv, s_send, s_recv, r_send, r_recv,
+    in_sem, cx_send, cx_recv, mx_send, mx_recv, c_send, c_recv, ag_send, ag_recv, mt_send, mt_recv, s_send, s_recv, r_send, r_recv,
     v_send, v_recv, p_send, p_recv, f_send, f_recv, g_send, g_recv,
 ):
     s = lax.axis_index("section")
@@ -113,15 +115,35 @@
     def g_summed(i):
         return remote(gpart.at[i], gparts.at[i], g_send.at[i], g_recv.at[i], device(s, z + AWAY[i], x))
 
-    own_in = pltpu.make_async_copy(x_in.at[0], tok.at[0, 0], in_sem.at[0])
-    own_grad = pltpu.make_async_copy(g_in.at[0], tok.at[0, 1], in_sem.at[1])
+    def cx_sent(xx):
+        return remote(cx.at[x], cx.at[x], cx_send.at[xx], cx_recv.at[x], device(s, z, xx))
+
+    def cx_arrived(xx):
+        return remote(cx.at[xx], cx.at[xx], cx_send.at[xx], cx_recv.at[xx], device(s, z, xx))
+
+    def mx_sent(xx):
+        return remote(mo.at[xx], mx.at[x], mx_send.at[xx], mx_recv.at[x], device(s, z, xx))
+
+    def mx_arrived(xx):
+        return remote(mo.at[x], mx.at[xx], mx_send.at[xx], mx_recv.at[xx], device(s, z, xx))
+
+    def crossed(i):
+        return remote(zs.at[i], gotc.at[i], c_send.at[i], c_recv.at[i], device(s, z - AWAY[i], x))
+
+    first, last = pl.ds(0, DA), pl.ds(DA, CW)
+    own = [
+        pltpu.make_async_copy(x_in.at[0, :, last], cx.at[x, 0], in_sem.at[5]),
+        pltpu.make_async_copy(g_in.at[0, :, last], cx.at[x, 1], in_sem.at[6]),
+        pltpu.make_async_copy(x_in.at[0, :, first], tok.at[0, 0], in_sem.at[0]),
+        pltpu.make_async_copy(g_in.at[0, :, first], tok.at[0, 1], in_sem.at[1]),
+    ]
     w_copies = [
         pltpu.make_async_copy(wg_in.at[0], wgu.at[:, :, pl.ds(0, H)], in_sem.at[2]),
         pltpu.make_async_copy(wu_in.at[0], wgu.at[:, :, pl.ds(H, H)], in_sem.at[3]),
         pltpu.make_async_copy(wd_in.at[0], wd, in_sem.at[4]),
     ]
-    own_in.start()
-    own_grad.start()
+    for c in own:
+        c.start()
 
     barrier = pltpu.get_barrier_semaphore()
 
@@ -150,7 +172,13 @@
         route = jnp.where(same, rtt[k : k + 1, :], route)
     before = jnp.where(iota((TOK, TOK), 0) < iota((TOK, TOK), 1), 1.0, 0.0).astype(BF16)
     slot = jnp.where(named > 0.5, dot(named.astype(BF16), before), -1.0)
-    meta[0] = jnp.where(row % 16 < 8, slot, route).astype(BF16)
+    table = jnp.where(row % 16 < 8, slot, route).astype(BF16)
+    meta[0] = table
+    taken = (row % 32) // 4 * 16 + (row % 4) // 2 * 8 + row // 32 * 2 + row % 2
+    moved = dot(jnp.where(taken == iota((TOK, TOK), 1), 1.0, 0.0).astype(BF16), table).astype(BF16)
+    for q in range(NX):
+        mo[q] = moved[32 * q : 32 * q + 32]
+    mx[x] = mo[x]
 
     def places(i):
         group = meta[i, pl.ds(pl.multiple_of(z * 16, 16), 16), :].astype(F32)
@@ -167,15 +195,31 @@
         if h == 0:
             places(i)
         which = place_w[i] if h else place[i]
-        for n in range(0, D, 256):
-            rows = dot(which, tok[i, h, :, n : n + 256]).astype(BF16)
+        for n in range(0, DA, 256):
+            m = min(n + 256, DA)
+            rows = dot(which, tok[i, h, :, n:m]).astype(BF16)
             for q in range(NX):
-                sel[i, q, h, :, n : n + 256] = rows[q * ROW : (q + 1) * ROW]
+                sel[i, q, h, :, n:m] = rows[q * ROW : (q + 1) * ROW]
 
     def send_chosen(i, h):
         for xx in others:
             sent(i, h, xx).start()
         got[i, x, h] = sel[i, x, h]
+
+    def cross(q):
+        mf[q] = mx[q].astype(F32)
+        place_of = iota((CAP, TOK), 0).astype(F32)
+        ones, routes = [], []
+        for i in range(NZ):
+            group = ((z + NZ - AWAY[i]) % NZ) * 4
+            for k in range(EL):
+                hit = mf[q, pl.ds(group + k, 1), :] == place_of
+                ones.append(jnp.where(hit, 1.0, 0.0))
+                routes.append(jnp.where(hit, mf[q, pl.ds(group + EL + k, 1), :], 0.0))
+        for h, pieces in ((0, ones), (1, routes)):
+            rows = dot(jnp.concatenate(pieces, axis=0).astype(BF16), cx[q, h]).astype(BF16)
+            for i in range(NZ):
+                zs[i, q, h] = rows[i * ROW : (i + 1) * ROW]
 
     def pass_on(i, h):
         if h == 0:
@@ -196,16 +240,23 @@
         for xx in others:
             for h in range(2):
                 arrived(i, h, xx).wait_recv()
+        if i:
+            crossed(i).wait_recv()
+        others_of = gotc if i else zs
         at = slice(i * SRC, (i + 1) * SRC)
-        wide = [got[i, q, 0].astype(F32) for q in range(NX)]
-        wide_w = [got[i, q, 1].astype(F32) for q in range(NX)]
+        wide = [[got[i, q, h].astype(F32) for q in range(NX)] for h in range(2)]
+        wide_c = [[others_of[i, q, h].astype(F32) for q in range(NX)] for h in range(2)]
         grads, vs = [], []
         for k in range(EL):
             mine = slice(k * CAP, (k + 1) * CAP)
-            rows = jnp.concatenate([w[mine] for w in wide], axis=0).astype(BF16)
-            weighted = jnp.concatenate([w[mine] for w in wide_w], axis=0).astype(BF16)
-            xs[k, at, :] = rows
-            ws[k, at, :] = weighted
+            both_of = []
+            for h, kept in ((0, xs), (1, ws)):
+                part_a = jnp.concatenate([w[mine] for w in wide[h]], axis=0).astype(BF16)
+                part_c = jnp.concatenate([w[mine] for w in wide_c[h]], axis=0).astype(BF16)
+                kept[k, at, 0:DA] = part_a
+                kept[k, at, DA:D] = part_c
+                both_of.append(jnp.concatenate([part_a, part_c], axis=1))
+            rows, weighted = both_of
             pre = dot(rows, wgu[k])
             gate, up = pre[:, :H], pre[:, H:]
             active_grad = dot_t(weighted, wd[k])
@@ -282,11 +333,14 @@
         else:
             down_out[0, k] = t_dot(act[k], ws[k]).astype(BF16)
 
-    own_in.wait()
-    own_grad.wait()
+    for c in own:
+        c.wait()
     chosen(0, 0)
     chosen(0, 1)
     pl.semaphore_wait(barrier, (NZ - 1) + (NX - 1) + 6)
+    for xx in others:
+        mx_sent(xx).start()
+        cx_sent(xx).start()
     mt(0, 1, below).start()
     mt(0, 2, above).start()
     for h in range(2):
@@ -301,39 +355,55 @@
         select(b, h)
 
     both(1, 2, 0)
-    both(1, 2, 1)
+    for xx in others:
+        mx_arrived(xx).wait_recv()
+        cx_arrived(xx).wait_recv()
+    cross(0)
+    cross(1)
+    pass_on(1, 1)
+    pass_on(2, 1)
+    select(1, 1)
+    select(2, 1)
+    cross(2)
+    cross(3)
     for c in w_copies:
         c.wait()
     expert_rows(0)
     both(3, 4, 0)
-    expert_rows(1)
     both(3, 4, 1)
-    expert_rows(2)
     both(5, 6, 0)
-    expert_rows(3)
     pass_on(5, 1)
     pass_on(6, 1)
+    for i in (7, 5, 6, 3, 4, 1, 2):
+        crossed(i).start()
     select(5, 1)
     pass_on(7, 0)
     pass_on(7, 1)
     select(7, 0)
     select(7, 1)
     select(6, 1)
-    expert_rows(4)
-    expert_rows(5)
     expert_rows(7)
     send_back(7)
+    expert_rows(5)
     send_back(5)
     expert_rows(6)
-    for i in (6, 3, 4, 1, 2, 0):
-        send_back(i)
+    send_back(6)
+    expert_rows(3)
+    send_back(3)
     combine(7)
+    expert_rows(4)
+    send_back(4)
+    combine(5)
+    expert_rows(1)
+    send_back(1)
+    expert_rows(2)
+    send_back(2)
+    send_back(0)
+    combine(6)
     update(0, 0)
-    combine(5)
     update(0, 1)
-    combine(6)
+    combine(3)
     update(0, 2)
-    combine(3)
     update(1, 0)
     combine(4)
     update(1, 1)
@@ -363,6 +433,7 @@
             for h in range(2):
                 ag(0, i, h, above).wait_send()
             g_summed(i).wait_send()
+            crossed(i).wait_send()
         for xx in others:
             for h in range(2):
                 sent(i, h, xx).wait_send()
@@ -370,6 +441,9 @@
             v_returned(i, xx).wait_send()
         for c in onward(i):
             c.wait_send()
+    for xx in others:
+        cx_sent(xx).wait_send()
+        mx_sent(xx).wait_send()
 
 
 def write_out(*refs):
@@ -394,12 +468,18 @@
         in_specs=[any_spec, any_spec, vmem, vmem, any_spec, any_spec, any_spec],
         out_specs=[vmem] * 5,
         scratch_shapes=[
-            pltpu.VMEM((NZ, 2, TOK, D), BF16),
+            pltpu.VMEM((NZ, 2, TOK, DA), BF16),
             pltpu.VMEM((NZ, TOK, TOK), BF16),
+            pltpu.VMEM((NX, 2, TOK, CW), BF16),
+            pltpu.VMEM((NX, 32, TOK), BF16),
+            pltpu.VMEM((NX, 32, TOK), BF16),
+            pltpu.VMEM((NX, 32, TOK), F32),
+            pltpu.VMEM((NZ, NX, 2, ROW, CW), BF16),
+            pltpu.VMEM((NZ, NX, 2, ROW, CW), BF16),
             pltpu.VMEM((NZ, ALL, TOK), BF16),
             pltpu.VMEM((NZ, ALL, TOK), BF16),
-            pltpu.VMEM((NZ, NX, 2, ROW, D), BF16),
-            pltpu.VMEM((NZ, NX, 2, ROW, D), BF16),
+            pltpu.VMEM((NZ, NX, 2, ROW, DA), BF16),
+            pltpu.VMEM((NZ, NX, 2, ROW, DA), BF16),
             pltpu.VMEM((EL, D, 2 * H), BF16),
             pltpu.VMEM((EL, H, D), BF16),
             pltpu.VMEM((EL, NZ * SRC, D), BF16),
@@ -415,7 +495,13 @@
             pltpu.VMEM((3, TOK, D), BF16),
             pltpu.VMEM((NZ, ER, TOK), F32),
             pltpu.VMEM((NZ, ER, TOK), F32),
-            dma((5,)),
+            dma((7,)),
+            dma((NX,)),
+            dma((NX,)),
+            dma((NX,)),
+            dma((NX,)),
+            dma((NZ,)),
+            dma((NZ,)),
             dma((NZ, 2)),
             dma((NZ, 2)),
             dma((NZ,)),

time: 130 us -> 118 us (0.908)
  Pallas kernels: 129 us -> 117 us
    pallas_call x1, Pallas kernels: 126 us -> 115 us  [body(): pl.pallas_call(kernel, name='layer_backward', out_shape=[pltpu.VMEM(shape...]
where the time goes in v4:
time: 118 us
  Pallas kernels  117 us (99%)
    pallas_call x1, Pallas kernels, body(): pl.pallas_call(kernel, name='layer_backward', out_shape=[pltpu.VMEM(shape...  115 us

profile of v4, /device:TPU:1, one launch (start us, length us, event | category | flops | bytes accessed | tf_op | source)
XLA Modules:
  0.0 118.0 jit_solution(982727706804195986)
XLA Ops:
  0.6 114.9 %layer_backward.1 = (bf16[1,128,1024]{2,1,0:T(8,128)(2,1)S(1)}, bf16[1,8,128]{2,1,0:T(8,128)(2,1)S(1)}, bf16[1,2,1024,384]{3,2,1,0:T(8,128)(2,1)S(1)}, bf16[1,2,...) custom-call(bf16[1,128,1024]{2,1,0:T(8,128)(2,1)} %x_in.1, bf16[1,128,1024]{2,1,0:T(8,128)(2,1)} %g_in.1, ...), custom_call_target="tpu_custom_call" | custom-call | flops 9663676416 | bytes 12582912 | tf_op jit(solution)/shard_map/layer_backward/pallas_call | solution.py:464
  115.5 2.3 %write_out.1 = (bf16[1,128,1024]{2,1,0:T(8,128)(2,1)}, bf16[1,8,128]{2,1,0:T(8,128)(2,1)}, bf16[1,2,1024,384]{3,2,1,0:T(8,128)(2,1)}, bf16[1,2,1024,384]{3,2,1,0:T(8,128)(2,1)}, bf16[1,2,384,1024]{3,2,1,0:T(8,128)(2,1)}) custom-call(bf16[1,128,1024]{2,1,0:T(8,128)(2,1)S(1)} %get-tuple-element.15.refs_0_, bf16[1,8,128]{2,1,0:T(8,128)(2,1)S(1)} %get-tuple-element.16.refs_1_, ...), custom_call_target="tpu_custom_call" | custom-call | bytes 5242880 | tf_op jit(solution)/shard_map/write_out/pallas_call | solution.py:527

commit v5 on v4

--- a/solution.py
+++ b/solution.py
@@ -16,6 +16,8 @@
 H = 384
 EL = 2
 CAP = 24
+NP = 2
+PC = D // NP
 ROW = EL * CAP
 ER = EL * NX
 ALL = NX * ROW
@@ -56,7 +58,7 @@
     x = e % NX
     s_prev = (s + NS - 1) % NS
     s_next = (s + 1) % NS
-    others = [(x + q) % NX for q in range(1, NX)]
+    others = [(x + q) % NX for q in (2, 1, 3)]
 
     def device(section, zz, xx):
         return {"section": section, "expert": ((zz + NZ) % NZ) * NX + xx}
@@ -84,33 +86,57 @@
             sel.at[i, x, h], got.at[i, xx, h], s_send.at[i, xx, h], s_recv.at[i, xx, h], device(s, z, xx)
         )
 
+    def spans(i):
+        return [(p, pl.ds(p * PC, PC)) for p in range(NP)] if i in (0, 1, 2) else [(0, pl.ds(0, D))]
+
     def returned(i, xx):
-        return remote(ret.at[i, xx], back.at[i, x], r_send.at[i, xx], r_recv.at[i, x], device(s, z, xx))
+        return [
+            remote(
+                ret.at[i, xx, :, c], back.at[i, x, :, c], r_send.at[i, xx, p], r_recv.at[i, x, p],
+                device(s, z, xx),
+            )
+            for p, c in spans(i)
+        ]
 
     def came_back(i, xx):
-        return remote(ret.at[i, x], back.at[i, xx], r_send.at[i, xx], r_recv.at[i, xx], device(s, z, xx))
-
-    def v_returned(i, xx):
-        return remote(vret.at[i], vback.at[i, x], v_send.at[i, xx], v_recv.at[i, x], device(s, z, xx))
-
-    def v_came_back(i, xx):
-        return remote(vret.at[i], vback.at[i, xx], v_send.at[i, xx], v_recv.at[i, xx], device(s, z, xx))
-
-    def onward(i):
-        if i == 7:
-            low, high = pl.ds(0, D // 2), pl.ds(D // 2, D // 2)
-            return [
-                remote(part.at[7, :, low], inc.at[5, :, low], p_send.at[5], p_recv.at[5], above),
-                remote(part.at[7, :, high], inc.at[6, :, high], p_send.at[6], p_recv.at[6], below),
-            ]
-        if i > 2:
-            to = above if i % 2 else below
-            return [remote(part.at[i], inc.at[i - 2], p_send.at[i - 2], p_recv.at[i - 2], to)]
-        to = device(s_prev, z + AWAY[i], x)
-        return [remote(part.at[i], fin.at[i], f_send.at[i], f_recv.at[i], to)]
-
-    def incoming(i):
-        return onward(7)[i - 5] if i > 4 else onward(i + 2)[0]
+        return [
+            remote(
+                ret.at[i, x, :, c], back.at[i, xx, :, c], r_send.at[i, xx, p], r_recv.at[i, xx, p],
+                device(s, z, xx),
+            )
+            for p, c in spans(i)
+        ]
+
+    def v_returned(xx):
+        return remote(vret, vback.at[x], v_send.at[xx], v_recv.at[x], device(s, z, xx))
+
+    def v_came_back(xx):
+        return remote(vret, vback.at[xx], v_send.at[xx], v_recv.at[xx], device(s, z, xx))
+
+    def onward(i, p):
+        cols = pl.ds(p * PC, PC)
+        if i < 3:
+            to = device(s_prev, z + AWAY[i], x)
+            return remote(
+                part.at[i, :, cols], fin.at[i, :, cols], f_send.at[i, p], f_recv.at[i, p], to
+            )
+        up = p < NP // 2 if i == 7 else i % 2 == 1
+        dst = (5 if up else 6) if i == 7 else i - 2
+        return remote(
+            part.at[i, :, cols], inc.at[dst, :, cols], p_send.at[dst, p], p_recv.at[dst, p],
+            above if up else below,
+        )
+
+    def pieces_in(i):
+        if i == 5:
+            return range(NP // 2)
+        if i == 6:
+            return range(NP // 2, NP)
+        return range(NP) if 0 < i < 5 else ()
+
+    def pieces(i):
+        upward = i % 2 == 1 and i != 7
+        return (*range(NP // 2, NP), *range(NP // 2)) if upward else range(NP)
 
     def g_summed(i):
         return remote(gpart.at[i], gparts.at[i], g_send.at[i], g_recv.at[i], device(s, z + AWAY[i], x))
@@ -287,42 +313,52 @@
         lines.append(jnp.zeros((8 - NX, TOK), F32))
         vret[i] = jnp.concatenate(lines, axis=0)
         back[i, x] = ret[i, x]
-        vback[i, x] = vret[i]
+        vback[x, i] = vret[i]
 
     def send_back(i):
+        for p in range(len(spans(i))):
+            for xx in others:
+                returned(i, xx)[p].start()
+
+    def send_v():
         for xx in others:
-            returned(i, xx).start()
-            v_returned(i, xx).start()
+            v_returned(xx).start()
 
     def combine(i):
+        one = place[i]
+        for count, p in enumerate(pieces(i)):
+            if count == 0 or len(spans(i)) > 1:
+                for xx in others:
+                    came_back(i, xx)[p if len(spans(i)) > 1 else 0].wait_recv()
+            if p in pieces_in(i):
+                onward(7 if i > 4 else i + 2, p).wait_recv()
+            for n in range(p * PC, (p + 1) * PC, 256):
+                rows = back[i, :, :, n : n + 256].reshape(ALL, 256)
+                total = t_dot(one, rows)
+                if p in pieces_in(i):
+                    total += inc[i, :, n : n + 256].astype(F32)
+                part[i, :, n : n + 256] = total.astype(BF16)
+            onward(i, p).start()
+    def routes():
         for xx in others:
-            came_back(i, xx).wait_recv()
-            v_came_back(i, xx).wait_recv()
-        if 0 < i < 7:
-            incoming(i).wait_recv()
-        one = place[i]
-        for n in range(0, D, 256):
-            rows = back[i, :, :, n : n + 256].reshape(ALL, 256)
-            total = t_dot(one, rows)
-            if 0 < i < 5 or (i == 5 and n < D // 2) or (i == 6 and n >= D // 2):
-                total += inc[i, :, n : n + 256].astype(F32)
-            part[i, :, n : n + 256] = total.astype(BF16)
-        for c in onward(i):
-            c.start()
-        lines = []
-        for q in range(NX):
-            line = vback[i, q, pl.ds(x, 1), :]
-            at_lane = iota((ROW, TOK), 1) == iota((ROW, TOK), 0)
-            column = jnp.sum(jnp.where(at_lane, line, 0.0), axis=1, keepdims=True)
-            spread = one[q * ROW : (q + 1) * ROW].astype(F32) * column
-            for k in range(EL):
-                lines.append(jnp.sum(spread[k * CAP : (k + 1) * CAP], axis=0, keepdims=True))
-        summed = jnp.concatenate(lines, axis=0)
-        if i:
-            gpart[i] = summed
-            g_summed(i).start()
-        else:
-            gparts[0] = summed
+            v_came_back(xx).wait_recv()
+        for i in range(1 - NZ, 1):
+            i = -i
+            one = place[i]
+            lines = []
+            for q in range(NX):
+                line = vback[q, i, pl.ds(x, 1), :]
+                at_lane = iota((ROW, TOK), 1) == iota((ROW, TOK), 0)
+                column = jnp.sum(jnp.where(at_lane, line, 0.0), axis=1, keepdims=True)
+                spread = one[q * ROW : (q + 1) * ROW].astype(F32) * column
+                for k in range(EL):
+                    lines.append(jnp.sum(spread[k * CAP : (k + 1) * CAP], axis=0, keepdims=True))
+            summed = jnp.concatenate(lines, axis=0)
+            if i:
+                gpart[i] = summed
+                g_summed(i).start()
+            else:
+                gparts[0] = summed
 
     def update(k, stage):
         if stage < 2:
@@ -388,15 +424,16 @@
     send_back(5)
     expert_rows(6)
     send_back(6)
+    combine(7)
     expert_rows(3)
     send_back(3)
-    combine(7)
     expert_rows(4)
     send_back(4)
     combine(5)
     expert_rows(1)
     send_back(1)
     expert_rows(2)
+    send_v()
     send_back(2)
     send_back(0)
     combine(6)
@@ -411,6 +448,7 @@
     update(1, 2)
     combine(2)
     combine(0)
+    routes()
 
     for i in range(1, NZ):
         g_summed(i).wait_recv()
@@ -423,7 +461,8 @@
     rg_out[0] = (acc / (lev_in[0].astype(F32) / 256.0)).astype(BF16)
 
     for i in range(3):
-        onward(i)[0].wait_recv()
+        for p in range(NP):
+            onward(i, p).wait_recv()
     total = fin[0].astype(F32) + fin[1].astype(F32) + fin[2].astype(F32)
     up_out[0] = jnp.where(s == NS - 1, 0.0, total).astype(BF16)
 
@@ -437,12 +476,13 @@
         for xx in others:
             for h in range(2):
                 sent(i, h, xx).wait_send()
-            returned(i, xx).wait_send()
-            v_returned(i, xx).wait_send()
-        for c in onward(i):
-            c.wait_send()
+            for c in returned(i, xx):
+                c.wait_send()
+        for p in range(NP):
+            onward(i, p).wait_send()
     for xx in others:
         cx_sent(xx).wait_send()
+        v_returned(xx).wait_send()
         mx_sent(xx).wait_send()
 
 
@@ -489,7 +529,7 @@
             pltpu.VMEM((NZ, NX, ROW, D), BF16),
             pltpu.VMEM((NZ, NX, ROW, D), BF16),
             pltpu.VMEM((NZ, 8, TOK), F32),
-            pltpu.VMEM((NZ, NX, 8, TOK), F32),
+            pltpu.VMEM((NX, NZ, 8, TOK), F32),
             pltpu.VMEM((NZ, TOK, D), BF16),
             pltpu.VMEM((NZ, TOK, D), BF16),
             pltpu.VMEM((3, TOK, D), BF16),
@@ -508,14 +548,14 @@
             dma((NZ,)),
             dma((NZ, NX, 2)),
             dma((NZ, NX, 2)),
-            dma((NZ, NX)),
-            dma((NZ, NX)),
-            dma((NZ, NX)),
-            dma((NZ, NX)),
-            dma((NZ,)),
-            dma((NZ,)),
-            dma((3,)),
-            dma((3,)),
+            dma((NZ, NX, NP)),
+            dma((NZ, NX, NP)),
+            dma((NX,)),
+            dma((NX,)),
+            dma((NZ, NP)),
+            dma((NZ, NP)),
+            dma((3, NP)),
+            dma((3, NP)),
             dma((NZ,)),
             dma((NZ,)),
         ],

time: 118 us -> 117 us (level)
  no operation moved by 1% of the time
where the time goes in v5:
time: 117 us
  Pallas kernels  116 us (99%)
    pallas_call x1, Pallas kernels, body(): pl.pallas_call(kernel, name='layer_backward', out_shape=[pltpu.VMEM(shape...  114 us

profile of v5, /device:TPU:1, one launch (start us, length us, event | category | flops | bytes accessed | tf_op | source)
XLA Modules:
  0.0 117.2 jit_solution(5656647111503153465)
XLA Ops:
  0.6 114.1 %layer_backward.1 = (bf16[1,128,1024]{2,1,0:T(8,128)(2,1)S(1)}, bf16[1,8,128]{2,1,0:T(8,128)(2,1)S(1)}, bf16[1,2,1024,384]{3,2,1,0:T(8,128)(2,1)S(1)}, bf16[1,2,...) custom-call(bf16[1,128,1024]{2,1,0:T(8,128)(2,1)} %x_in.1, bf16[1,128,1024]{2,1,0:T(8,128)(2,1)} %g_in.1, ...), custom_call_target="tpu_custom_call" | custom-call | flops 9663676416 | bytes 12582912 | tf_op jit(solution)/shard_map/layer_backward/pallas_call | solution.py:504
  114.7 2.3 %write_out.1 = (bf16[1,128,1024]{2,1,0:T(8,128)(2,1)}, bf16[1,8,128]{2,1,0:T(8,128)(2,1)}, bf16[1,2,1024,384]{3,2,1,0:T(8,128)(2,1)}, bf16[1,2,1024,384]{3,2,1,0:T(8,128)(2,1)}, bf16[1,2,384,1024]{3,2,1,0:T(8,128)(2,1)}) custom-call(bf16[1,128,1024]{2,1,0:T(8,128)(2,1)S(1)} %get-tuple-element.15.refs_0_, bf16[1,8,128]{2,1,0:T(8,128)(2,1)S(1)} %get-tuple-element.16.refs_1_, ...), custom_call_target="tpu_custom_call" | custom-call | bytes 5242880 | tf_op jit(solution)/shard_map/write_out/pallas_call | solution.py:567
